TPU v7x, 32 devices: a 4x4x1 block of a 4x4x8 slice. The times are simulated.
32 devices in a mesh: dp: 1 (over z), sx: 4 (over y), sy: 8 (over x, core).
Axes of the slice: x: 4, y: 4, z: 1, core: 2. Of those that a mesh axis runs over, the one named last changes fastest.
The devices are a block of a 4x4x8 slice.
Arguments:
- act_in: bfloat16 [4, 512, 64, 256], P('dp', 'sy', 'sx')
- norm_first: bfloat16 [2, 256], replicated
- w_first: bfloat16 [3, 3, 256, 128], replicated
- w_short: bfloat16 [256, 128], replicated
- norm_rest: bfloat16 [6, 2, 128], replicated
- w_rest: bfloat16 [5, 3, 3, 128, 128], replicated
- bias_rest: bfloat16 [7, 128], replicated
- w_out: bfloat16 [3, 3, 128, 3], replicated
- bias_out: bfloat16 [3], replicated
Outputs:
- output: float32 [4, 512, 64, 3], P('dp', 'sy', 'sx')
All inputs are finite; a program needn't handle non-finite values.
Results may differ from a plain program's by a relative error of at most 0.0121751.
Values are sent between devices in bfloat16 or wider.
A program may use at most 768 MiB of HBM per device.

v0:
```python
import jax
import jax.numpy as jnp
from jax import lax
from jax.sharding import PartitionSpec as P

GROUPS = 32
GN_EPS = 1e-6


def solution(mesh):
    rows_n = mesh.shape["sy"]
    cols_n = mesh.shape["sx"]
    to_below = [(position, position + 1) for position in range(rows_n - 1)]
    to_above = [(position + 1, position) for position in range(rows_n - 1)]
    to_right = [(position, position + 1) for position in range(cols_n - 1)]
    to_left = [(position + 1, position) for position in range(cols_n - 1)]
    tile_spec = P("dp", "sy", "sx", None)
    replicated = P()

    def add_border(act_map):
        top_row = lax.ppermute(act_map[:, -1:], "sy", to_below)
        bottom_row = lax.ppermute(act_map[:, :1], "sy", to_above)
        tall = jnp.concatenate([top_row, act_map, bottom_row], axis=1)
        left_col = lax.ppermute(tall[:, :, -1:], "sx", to_right)
        right_col = lax.ppermute(tall[:, :, :1], "sx", to_left)
        return jnp.concatenate([left_col, tall, right_col], axis=2)

    def conv_tile(act_map, kernel):
        return lax.conv_general_dilated(add_border(act_map), kernel, (1, 1), ((0, 0), (0, 0)), dimension_numbers=("NHWC", "HWIO", "NHWC"), preferred_element_type=jnp.float32)

    def group_norm_act(act_map, norm_pair):
        samples = act_map.shape[0]
        per_group = act_map.shape[3] // GROUPS
        group_count = act_map.shape[1] * rows_n * act_map.shape[2] * cols_n * per_group
        sum_one = jnp.sum(act_map, axis=(1, 2), dtype=jnp.float32).reshape(samples, GROUPS, per_group).sum(axis=2)
        sum_two = jnp.sum(jnp.square(act_map.astype(jnp.float32)), axis=(1, 2)).reshape(samples, GROUPS, per_group).sum(axis=2)
        totals = lax.psum(jnp.stack([sum_one, sum_two], axis=-1), ("sy", "sx"))
        group_mean = totals[:, :, 0] / group_count
        inv_std = lax.rsqrt(totals[:, :, 1] / group_count - group_mean * group_mean + GN_EPS)
        chan_scale = jnp.repeat(inv_std, per_group, axis=1) * norm_pair[0].astype(jnp.float32)
        chan_shift = norm_pair[1].astype(jnp.float32) - jnp.repeat(group_mean, per_group, axis=1) * chan_scale
        return jax.nn.silu(act_map.astype(jnp.float32) * chan_scale[:, None, None, :] + chan_shift[:, None, None, :]).astype(jnp.bfloat16)

    def local_decode(act_in, norm_first, w_first, w_short, norm_rest, w_rest, bias_rest, w_out, bias_out):
        bias_rows = bias_rest.astype(jnp.float32)
        mid_act = (conv_tile(group_norm_act(act_in, norm_first), w_first) + bias_rows[0]).astype(jnp.bfloat16)
        skip_path = jnp.einsum("nhwc,cd->nhwd", act_in, w_short, preferred_element_type=jnp.float32) + bias_rows[6]
        hidden = (conv_tile(group_norm_act(mid_act, norm_rest[0]), w_rest[0]) + bias_rows[1] + skip_path).astype(jnp.bfloat16)
        for res_index in range(1, 3):
            first_at = 2 * res_index - 1
            mid_act = (conv_tile(group_norm_act(hidden, norm_rest[first_at]), w_rest[first_at]) + bias_rows[first_at + 1]).astype(jnp.bfloat16)
            hidden = (conv_tile(group_norm_act(mid_act, norm_rest[first_at + 1]), w_rest[first_at + 1]) + bias_rows[first_at + 2] + hidden.astype(jnp.float32)).astype(jnp.bfloat16)
        return conv_tile(group_norm_act(hidden, norm_rest[5]), w_out) + bias_out.astype(jnp.float32)

    return jax.shard_map(local_decode, mesh=mesh, in_specs=(tile_spec, replicated, replicated, replicated, replicated, replicated, replicated, replicated, replicated), out_specs=tile_spec, check_vma=False)
```

profile of v0, /device:TPU:97, one launch (start us, length us, event | category | flops | bytes accessed | tf_op | source)
XLA Modules:
  0.0 574.9 jit_solution(9693462241800392380)
XLA Ops:
  2.9 49.8 %psum.49 = f32[4,32,2]{1,0,2:T(4,128)S(1)} all-reduce(f32[4,32,2]{1,0,2:T(4,128)S(1)} %pad_maximum_fusion.21), channel_id=1, replica_groups=mesh['dp'=1,'sx'=4,'sy'=8] {'sy','sx'}, use_global_device_ids=true, to_apply=%region_4.0 | all-reduce | flops 256 | bytes 2048 | tf_op jit(solution)/shard_map/psum | solution.py:37
  59.9 3.1 collective-permute-done.1
  67.6 3.8 collective-permute-done.3
  76.5 6.5 %fusion.1 = bf16[66,4,8,5,256]{4,1,3,2,0:T(4,128)(2,1)S(1)} fusion(bf16[66,4,7,2,256]{4,1,3,2,0:T(4,128)(2,1)S(1)} %slice.338, bf16[66,4,8,3,256]{4,1,3,2,0:T(4,128)(2,1)S(1)} %bitcast.298), kind=kLoop, calls=%fused_computation.5 | loop fusion | flops 16220160 | bytes 10543104 | tf_op jit(solution)/shard_map/conv_general_dilated | solution.py:29
  83.1 9.5 %fusion.143 = (f32[64,32,3,128]{3,1,2,0:T(8,128)}, f32[64,32,3,128]{3,1,2,0:T(8,128)S(1)}) fusion(f32[128]{0:T(128)S(1)} %get-tuple-element.63, bf16[3,3,256,128]{3,2,1,0:T(8,128)(2,1)S(1)} %copy-done, bf16[66,4,8,5,256]{4,1,3,2,0:T(4,128)(2,1)S(1)} %fusion.1, pred[32,3]{0,1:T(4,128)(4,1)S(1)} %copy-done.11), kind=kOutput, calls=%fused_computation.262 | convolution fusion | flops 3627810816 | bytes 12288608 | tf_op jit(solution)/shard_map/conv_general_dilated | solution.py:29
  94.8 3.7 copy.164
  99.1 45.2 %psum.50 = f32[4,32,2]{1,0,2:T(4,128)S(1)} all-reduce(f32[4,32,2]{1,0,2:T(4,128)S(1)} %pad_maximum_fusion.22), channel_id=1, replica_groups=mesh['dp'=1,'sx'=4,'sy'=8] {'sy','sx'}, use_global_device_ids=true, to_apply=%region_9.10 | all-reduce | flops 256 | bytes 2048 | tf_op jit(solution)/shard_map/psum | solution.py:37
  146.7 3.9 multiply_convert_fusion.2
  155.1 3.0 collective-permute-start.4
  163.5 4.0 collective-permute-done.7
  170.9 4.9 select_add_fusion.2
  181.6 44.8 %psum.51 = f32[4,32,2]{1,0,2:T(4,128)S(1)} all-reduce(f32[4,32,2]{1,0,2:T(4,128)S(1)} %pad_maximum_fusion.23), channel_id=1, replica_groups=mesh['dp'=1,'sx'=4,'sy'=8] {'sy','sx'}, use_global_device_ids=true, to_apply=%region_14.15 | all-reduce | flops 256 | bytes 2048 | tf_op jit(solution)/shard_map/psum | solution.py:37
  240.4 4.0 collective-permute-done.11
  248.1 6.5 %fusion.144 = (f32[64,32,3,128]{3,1,2,0:T(8,128)}, f32[64,32,3,128]{3,1,2,0:T(8,128)S(1)}) fusion(f32[128]{0:T(128)S(1)} %get-tuple-element.60, bf16[5,3,3,128,128]{4,3,2,1,0:T(8,128)(2,1)} %param.14, bf16[66,4,8,5,128]{4,1,3,2,0:T(4,128)(2,1)S(1)} %fusion.20, pred[32,3]{0,1:T(4,128)(4,1)S(1)} %copy-done.11), kind=kOutput, calls=%fused_computation.263 | convolution fusion | flops 1815871488 | bytes 9290336 | tf_op jit(solution)/shard_map/conv_general_dilated | solution.py:29
  256.8 3.7 copy.179
  261.0 45.2 %psum.52 = f32[4,32,2]{1,0,2:T(4,128)S(1)} all-reduce(f32[4,32,2]{1,0,2:T(4,128)S(1)} %pad_maximum_fusion.24), channel_id=1, replica_groups=mesh['dp'=1,'sx'=4,'sy'=8] {'sy','sx'}, use_global_device_ids=true, to_apply=%region_19.20 | all-reduce | flops 256 | bytes 2048 | tf_op jit(solution)/shard_map/psum | solution.py:37
  307.3 4.0 multiply_convert_fusion.1
  314.7 3.0 collective-permute-start.12
  322.4 4.0 collective-permute-done.15
  329.7 4.9 select_add_fusion.1
  339.4 45.1 %psum.53 = f32[4,32,2]{1,0,2:T(4,128)S(1)} all-reduce(f32[4,32,2]{1,0,2:T(4,128)S(1)} %pad_maximum_fusion.25), channel_id=1, replica_groups=mesh['dp'=1,'sx'=4,'sy'=8] {'sy','sx'}, use_global_device_ids=true, to_apply=%region_24.25 | all-reduce | flops 256 | bytes 2048 | tf_op jit(solution)/shard_map/psum | solution.py:37
  397.6 4.0 collective-permute-done.19
  405.3 6.5 %fusion.145 = (f32[64,32,3,128]{3,1,2,0:T(8,128)}, f32[64,32,3,128]{3,1,2,0:T(8,128)S(1)}) fusion(f32[128]{0:T(128)S(1)} %get-tuple-element.57, bf16[5,3,3,128,128]{4,3,2,1,0:T(8,128)(2,1)} %param.14, bf16[66,4,8,5,128]{4,1,3,2,0:T(4,128)(2,1)S(1)} %fusion.22, pred[32,3]{0,1:T(4,128)(4,1)S(1)} %copy-done.11), kind=kOutput, calls=%fused_computation.264 | convolution fusion | flops 1815871488 | bytes 9290336 | tf_op jit(solution)/shard_map/conv_general_dilated | solution.py:29
  414.1 3.7 copy.194
  418.2 45.3 %psum.54 = f32[4,32,2]{1,0,2:T(4,128)S(1)} all-reduce(f32[4,32,2]{1,0,2:T(4,128)S(1)} %pad_maximum_fusion.26), channel_id=1, replica_groups=mesh['dp'=1,'sx'=4,'sy'=8] {'sy','sx'}, use_global_device_ids=true, to_apply=%region_29.30 | all-reduce | flops 256 | bytes 2048 | tf_op jit(solution)/shard_map/psum | solution.py:37
  464.7 4.0 multiply_convert_fusion
  469.4 2.9 collective-permute-start.21
  479.7 4.0 collective-permute-done.23
  487.0 4.9 select_add_fusion
  496.7 45.7 %psum.55 = f32[4,32,2]{1,0,2:T(4,128)S(1)} all-reduce(f32[4,32,2]{1,0,2:T(4,128)S(1)} %pad_maximum_fusion.27), channel_id=1, replica_groups=mesh['dp'=1,'sx'=4,'sy'=8] {'sy','sx'}, use_global_device_ids=true, to_apply=%region_34.35 | all-reduce | flops 256 | bytes 2048 | tf_op jit(solution)/shard_map/psum | solution.py:37
  555.4 4.0 collective-permute-done.27
  563.1 10.2 %fusion.25 = f32[64,32,3,3]{1,3,2,0:T(4,128)S(1)} fusion(bf16[3,3,128,3]{2,3,1,0:T(4,128)(2,1)S(1)} %copy-done.12, bf16[66,4,8,5,128]{4,1,3,2,0:T(4,128)(2,1)S(1)} %fusion.24), kind=kOutput, calls=%fused_computation.56 | convolution fusion | flops 42467328 | bytes 2784000 | tf_op jit(solution)/shard_map/conv_general_dilated | solution.py:29
  (275 shorter events, 134.9 us)
Async XLA Ops:
  0.0 83.1 %copy-start = (bf16[3,3,256,128]{3,2,1,0:T(8,128)(2,1)S(1)}, bf16[3,3,256,128]{3,2,1,0:T(8,128)(2,1)}, u32[]{:S(2)}) copy-start(bf16[3,3,256,128]{3,2,1,0:T(8,128)(2,1)} %param.11) | copy-start | bytes 1769476
  2.5 57.4 %copy-start.10 = (bf16[7,128]{1,0:T(8,128)(2,1)S(1)}, bf16[7,128]{1,0:T(8,128)(2,1)}, u32[]{:S(2)}) copy-start(bf16[7,128]{1,0:T(8,128)(2,1)} %param.15) | copy-start | bytes 5380
  55.5 4.4 collective-permute-start
  57.4 5.6 collective-permute-start.1
  63.1 4.5 collective-permute-start.2
  65.6 5.9 %collective-permute-start.3 = (bf16[4,66,1,256]{3,1,2,0:T(8,128)(2,1)S(1)}, bf16[4,66,1,256]{3,1,2,0:T(8,128)(2,1)S(1)}, u32[]{:S(2)}, u32[]{:S(2)}) collective-permute-start(bf16[4,66,1,256]{3,1,2,0:T(8,128)(2,1)S(1)} %get-tuple-element.30), channel_id=1, source_target_pairs={{8,0},{16,8},{24,16},{9,1},{17,9},{25,17},{10,2},{18,10},{26,18},{... | collective-permute-start | bytes 405512 | tf_op jit(solution)/shard_map/ppermute | solution.py:25
  152.4 7.1 %collective-permute-start.5 = (bf16[4,1,16,128]{3,1,2,0:T(2,128)(2,1)S(1)}, bf16[4,1,16,128]{3,1,2,0:T(2,128)(2,1)S(1)}, u32[]{:S(2)}, u32[]{:S(2)}) collective-permute-start(bf16[4,1,16,128]{3,1,2,0:T(2,128)(2,1)S(1)} %copy.170), channel_id=1, source_target_pairs={{1,0},{2,1},{3,2},{4,3},{5,4},{6,5},{7,6},{9,8},{10,9},{11,10},{12... | collective-permute-start | bytes 49160 | tf_op jit(solution)/shard_map/ppermute | solution.py:22
  155.1 4.4 collective-permute-start.4
  159.6 3.9 collective-permute-start.6
  161.4 6.0 %collective-permute-start.7 = (bf16[4,66,1,128]{3,1,2,0:T(8,128)(2,1)S(1)}, bf16[4,66,1,128]{3,1,2,0:T(8,128)(2,1)S(1)}, u32[]{:S(2)}, u32[]{:S(2)}) collective-permute-start(bf16[4,66,1,128]{3,1,2,0:T(8,128)(2,1)S(1)} %get-tuple-element.44), channel_id=1, source_target_pairs={{8,0},{16,8},{24,16},{9,1},{17,9},{25,17},{10,2},{18,10},{26,18},{... | collective-permute-start | bytes 202760 | tf_op jit(solution)/shard_map/ppermute | solution.py:25
  228.7 4.4 collective-permute-start.8
  230.7 5.1 collective-permute-start.9
  236.0 4.4 collective-permute-start.10
  238.4 6.0 %collective-permute-start.11 = (bf16[4,66,1,128]{3,2,1,0:T(2,128)(2,1)S(1)}, bf16[4,66,1,128]{3,2,1,0:T(2,128)(2,1)S(1)}, u32[]{:S(2)}, u32[]{:S(2)}) collective-permute-start(bf16[4,66,1,128]{3,2,1,0:T(2,128)(2,1)S(1)} %get-tuple-element.50), channel_id=1, source_target_pairs={{8,0},{16,8},{24,16},{9,1},{17,9},{25,17},{10,2},{18,10},{26,18},{... | collective-permute-start | bytes 202760 | tf_op jit(solution)/shard_map/ppermute | solution.py:25
  312.0 6.6 %collective-permute-start.13 = (bf16[4,1,16,128]{3,1,2,0:T(2,128)(2,1)S(1)}, bf16[4,1,16,128]{3,1,2,0:T(2,128)(2,1)S(1)}, u32[]{:S(2)}, u32[]{:S(2)}) collective-permute-start(bf16[4,1,16,128]{3,1,2,0:T(2,128)(2,1)S(1)} %copy.185), channel_id=1, source_target_pairs={{1,0},{2,1},{3,2},{4,3},{5,4},{6,5},{7,6},{9,8},{10,9},{11,10},{12... | collective-permute-start | bytes 49160 | tf_op jit(solution)/shard_map/ppermute | solution.py:22
  314.7 3.9 collective-permute-start.12
  318.7 3.8 collective-permute-start.14
  320.4 6.0 %collective-permute-start.15 = (bf16[4,66,1,128]{3,1,2,0:T(8,128)(2,1)S(1)}, bf16[4,66,1,128]{3,1,2,0:T(8,128)(2,1)S(1)}, u32[]{:S(2)}, u32[]{:S(2)}) collective-permute-start(bf16[4,66,1,128]{3,1,2,0:T(8,128)(2,1)S(1)} %get-tuple-element.42), channel_id=1, source_target_pairs={{8,0},{16,8},{24,16},{9,1},{17,9},{25,17},{10,2},{18,10},{26,18},{... | collective-permute-start | bytes 202760 | tf_op jit(solution)/shard_map/ppermute | solution.py:25
  339.0 63.7 %copy-start.5 = (bf16[4,64,16,128]{3,2,1,0:T(8,128)(2,1)}, bf16[4,64,16,128]{3,2,1,0:T(8,128)(2,1)S(1)}, u32[]{:S(2)}) copy-start(bf16[4,64,16,128]{3,2,1,0:T(8,128)(2,1)S(1)} %get-tuple-element.20) | copy-start | bytes 3145732
  385.6 4.8 collective-permute-start.16
  387.5 5.5 collective-permute-start.17
  393.3 4.4 collective-permute-start.18
  395.7 6.0 %collective-permute-start.19 = (bf16[4,66,1,128]{3,2,1,0:T(2,128)(2,1)S(1)}, bf16[4,66,1,128]{3,2,1,0:T(2,128)(2,1)S(1)}, u32[]{:S(2)}, u32[]{:S(2)}) collective-permute-start(bf16[4,66,1,128]{3,2,1,0:T(2,128)(2,1)S(1)} %get-tuple-element.48), channel_id=1, source_target_pairs={{8,0},{16,8},{24,16},{9,1},{17,9},{25,17},{10,2},{18,10},{26,18},{... | collective-permute-start | bytes 202760 | tf_op jit(solution)/shard_map/ppermute | solution.py:25
  469.4 6.6 %collective-permute-start.21 = (bf16[4,1,16,128]{3,1,2,0:T(2,128)(2,1)S(1)}, bf16[4,1,16,128]{3,1,2,0:T(2,128)(2,1)S(1)}, u32[]{:S(2)}, u32[]{:S(2)}) collective-permute-start(bf16[4,1,16,128]{3,1,2,0:T(2,128)(2,1)S(1)} %copy.200), channel_id=1, source_target_pairs={{1,0},{2,1},{3,2},{4,3},{5,4},{6,5},{7,6},{9,8},{10,9},{11,10},{12... | collective-permute-start | bytes 49160 | tf_op jit(solution)/shard_map/ppermute | solution.py:22
  472.4 3.6 collective-permute-start.20
  476.1 3.7 collective-permute-start.22
  477.7 6.0 %collective-permute-start.23 = (bf16[4,66,1,128]{3,1,2,0:T(8,128)(2,1)S(1)}, bf16[4,66,1,128]{3,1,2,0:T(8,128)(2,1)S(1)}, u32[]{:S(2)}, u32[]{:S(2)}) collective-permute-start(bf16[4,66,1,128]{3,1,2,0:T(8,128)(2,1)S(1)} %get-tuple-element.40), channel_id=1, source_target_pairs={{8,0},{16,8},{24,16},{9,1},{17,9},{25,17},{10,2},{18,10},{26,18},{... | collective-permute-start | bytes 202760 | tf_op jit(solution)/shard_map/ppermute | solution.py:25
  496.2 58.5 %copy-start.13 = (bf16[3]{0:T(256)(128)(2,1)S(1)}, bf16[3]{0:T(256)(128)(2,1)}, u32[]{:S(2)}) copy-start(bf16[3]{0:T(256)(128)(2,1)} %param.17) | copy-start | bytes 22
  543.5 4.7 collective-permute-start.24
  545.4 5.3 collective-permute-start.25
  551.0 4.4 collective-permute-start.26
  553.4 6.0 %collective-permute-start.27 = (bf16[4,66,1,128]{3,2,1,0:T(2,128)(2,1)S(1)}, bf16[4,66,1,128]{3,2,1,0:T(2,128)(2,1)S(1)}, u32[]{:S(2)}, u32[]{:S(2)}) collective-permute-start(bf16[4,66,1,128]{3,2,1,0:T(2,128)(2,1)S(1)} %get-tuple-element.46), channel_id=1, source_target_pairs={{8,0},{16,8},{24,16},{9,1},{17,9},{25,17},{10,2},{18,10},{26,18},{... | collective-permute-start | bytes 202760 | tf_op jit(solution)/shard_map/ppermute | solution.py:25
  (10 other events, 94.3 us)
where the time goes:
time: 584 us; the launch traced here: 575 us
  blocking collectives  321 us (55%)
  starting transfers between devices  60 us (10%)
  local copies, waits for them, and re-layouts  50.7 us (9%)
  matrix products  50.1 us (9%)
  other arithmetic  46.4 us (8%)
  waiting for transfers between devices  44.5 us (8%)
    psum x7, blocking collectives, group_norm_act(): totals = lax.psum(jnp.stack([sum_one, sum_two], axis=-1), ('sy', 'sx'))  321 us
    conv_general_dilated x7, matrix products, conv_tile(): lax.conv_general_dilated(add_border(act_map), kernel, (1, 1), ((0, 0), (0...  47.4 us
    ppermute x7, waiting for transfers between devices, add_border(): right_col = lax.ppermute(tall[:, :, :1], 'sx', to_left)  27.9 us
    ppermute x7, starting transfers between devices, add_border(): bottom_row = lax.ppermute(act_map[:, :1], 'sy', to_above)  18.5 us
    ppermute x7, starting transfers between devices, add_border(): top_row = lax.ppermute(act_map[:, -1:], 'sy', to_below)  16.5 us
    convert_element_type x7, other arithmetic, group_norm_act(): jax.nn.silu(act_map.astype(jnp.float32) * chan_scale[:, None, None, :] +...  16.3 us
    ppermute x7, starting transfers between devices, add_border(): left_col = lax.ppermute(tall[:, :, -1:], 'sx', to_right)  14.9 us
    conv_general_dilated x7, other arithmetic, conv_tile(): lax.conv_general_dilated(add_border(act_map), kernel, (1, 1), ((0, 0), (0...  14.2 us
  transfers between devices with their start and end apart: 28, of which 20 were waited for; matrix products, arithmetic and copies ran while one was open for 0% of the time, Pallas kernels for 0%

commit v1 on v0

v1 whole, which is shorter than its diff:
```python
import functools

import jax
import jax.numpy as jnp
from jax import lax
from jax.experimental import pallas as pl
from jax.experimental.pallas import tpu as pltpu
from jax.sharding import PartitionSpec as P

GROUPS = 32
GN_EPS = 1e-6
MESH = pl.DeviceIdType.MESH
LANES = 128
ROW_BLOCK = 8
LAYERS = 7


def group_total(vec, per_group):
    lane = lax.broadcasted_iota(jnp.int32, vec.shape, 1)
    step = 1
    while step < per_group:
        low = pltpu.roll(vec, LANES - step, 1)
        high = pltpu.roll(vec, step, 1)
        vec = vec + jnp.where((lane & step) == 0, low, high)
        step *= 2
    return vec


def decode_kernel(rows_n, cols_n, act_hbm, norm_first, wf_hbm, ws_hbm, norm_rest, wr_hbm, bias_rest, wo_ref, bias_out, y_ref,
                  act, wf, ws, wr, wo, mid, hid, skip, pad_first, pad_rest, slab, edge_l, edge_r, turn,
                  st_first, st_rest, row_first, row_rest, col_first, col_rest,
                  cs_first, cs_rest, rs_rest,
                  load_sem, st_recv, row_recv, col_recv, st_send, row_send, col_send):
    samples, rows, cols, _ = act.shape
    pairs = rows // 2
    peers_n = rows_n * cols_n
    sx, sy = lax.axis_index("sx"), lax.axis_index("sy")
    at_x = [sx] + [lax.rem(sx + off, cols_n) for off in range(1, cols_n)]
    at_y = [sy] + [lax.rem(sy + off, rows_n) for off in range(1, rows_n)]
    peers = [{"sx": at_x[off // rows_n], "sy": at_y[off % rows_n]} for off in range(1, peers_n)]
    left, right, above, below = at_x[cols_n - 1], at_x[1], at_y[rows_n - 1], at_y[1]
    has_l, has_r, has_t, has_b = sx > 0, sx < cols_n - 1, sy > 0, sy < rows_n - 1

    loads = [pltpu.make_async_copy(act_hbm.at[s], act.at[s], load_sem.at[s]) for s in range(samples)]
    loads.append(pltpu.make_async_copy(ws_hbm, ws, load_sem.at[samples]))
    loads.append(pltpu.make_async_copy(wf_hbm, wf, load_sem.at[samples + 1]))
    loads.append(pltpu.make_async_copy(wr_hbm, wr, load_sem.at[samples + 2]))
    for load in loads:
        load.start()
    barrier = pltpu.get_barrier_semaphore()
    for peer in peers:
        pl.semaphore_signal(barrier, inc=1, device_id=peer, device_id_type=MESH)

    def stat_ref(layer):
        return st_first if layer == 0 else st_rest.at[layer - 1]

    def row_ref(layer):
        return row_first if layer == 0 else row_rest.at[layer - 1]

    def col_ref(layer):
        return col_first if layer == 0 else col_rest.at[layer - 1]

    def remote(src, dst, send, recv, peer):
        pltpu.make_async_remote_copy(src_ref=src, dst_ref=dst, send_sem=send, recv_sem=recv, device_id=peer, device_id_type=MESH).start()

    def send_all(layer, s, sums):
        stats = stat_ref(layer)
        for at, part in enumerate(sums):
            stats[s, 0, :, at * LANES:(at + 1) * LANES] = part
        for slot, peer in enumerate(peers):
            remote(stats.at[s, 0], stats.at[s, slot + 1], st_send.at[layer], st_recv.at[layer, s], peer)
        top = act.at[s, 0] if layer == 0 else rs_rest.at[layer - 1, s, 0]
        bottom = act.at[s, rows - 1] if layer == 0 else rs_rest.at[layer - 1, s, 1]
        col_src = cs_first.at[s] if layer == 0 else cs_rest.at[layer - 1, s]
        halo_rows, halo_cols = row_ref(layer), col_ref(layer)
        for src, y_to, base in ((top, above, 3), (bottom, below, 0)):
            for x_to, at in ((sx, 1), (left, 2), (right, 0)):
                remote(src, halo_rows.at[s, base + at], row_send.at[layer], row_recv.at[layer, s], {"sx": x_to, "sy": y_to})
        remote(col_src.at[0], halo_cols.at[s, 1], col_send.at[layer], col_recv.at[layer, s], {"sx": left, "sy": sy})
        remote(col_src.at[1], halo_cols.at[s, 0], col_send.at[layer], col_recv.at[layer, s], {"sx": right, "sy": sy})

    def wait_for(ref, sem):
        pltpu.make_async_copy(ref, ref, sem).wait()

    sub = lax.broadcasted_iota(jnp.int32, (8, LANES), 0)
    first_sub, last_sub = sub == 0, sub == 7

    def affine(layer, s):
        stats = stat_ref(layer)
        norm = norm_first if layer == 0 else norm_rest.at[layer - 1]
        channels = stats.shape[-1]
        per_group = channels // GROUPS
        count = rows * rows_n * cols * cols_n * per_group
        total = jnp.sum(stats[s], axis=0)
        pair = norm[...].astype(jnp.float32)
        out = []
        for at in range(channels // LANES):
            lanes = slice(at * LANES, (at + 1) * LANES)
            mean = group_total(jnp.broadcast_to(total[0:1, lanes], (8, LANES)), per_group) / count
            square = group_total(jnp.broadcast_to(total[1:2, lanes], (8, LANES)), per_group) / count
            scale = lax.rsqrt(square - mean * mean + GN_EPS) * jnp.broadcast_to(pair[0:1, lanes], (8, LANES))
            shift = jnp.broadcast_to(pair[1:2, lanes], (8, LANES)) - mean * scale
            out.append((0.5 * scale, 0.5 * shift))
        return out

    def silu(x, half_scale, half_shift):
        u = x * half_scale + half_shift
        return u + u * jnp.tanh(u)

    def activate(layer, s, pad, row_source, place):
        wait_for(stat_ref(layer).at[s, pl.ds(1, peers_n - 1)], st_recv.at[layer, s])
        scales = affine(layer, s)
        wait_for(row_ref(layer).at[s], row_recv.at[layer, s])
        wait_for(col_ref(layer).at[s], col_recv.at[layer, s])
        halo_rows, halo_cols = row_ref(layer), col_ref(layer)

        def store(v0, v1, from_left, from_right, tile, pair_at, half):
            r0, r1 = pltpu.roll(v0, 1, 0), pltpu.roll(v1, 1, 0)
            q0, q1 = pltpu.roll(v0, 7, 0), pltpu.roll(v1, 7, 0)
            shifted = (
                (jnp.where(first_sub, from_left, r0), jnp.where(first_sub, r0, r1)),
                (v0, v1),
                (jnp.where(last_sub, q1, q0), jnp.where(last_sub, from_right, q1)),
            )
            for off in range(3):
                place(pad, off, tile, pair_at, half, jnp.concatenate(shifted[off], axis=0).astype(jnp.bfloat16))

        for tile, (hs, ht) in enumerate(scales):
            lanes = slice(tile * LANES, (tile + 1) * LANES)
            edge_l[...] = jnp.where(has_l, silu(halo_cols[s, 0, :, lanes].astype(jnp.float32), hs[0:1], ht[0:1]), 0.0)
            edge_r[...] = jnp.where(has_r, silu(halo_cols[s, 1, :, lanes].astype(jnp.float32), hs[0:1], ht[0:1]), 0.0)
            for base, has, pair_at, half in ((0, has_t, 0, 0), (3, has_b, pairs, 1)):
                def halo(at):
                    row = halo_rows[s, base + at, :, lanes].astype(jnp.float32)
                    return silu(row[0:8], hs, ht), silu(row[8:16], hs, ht)

                corner_l = jnp.where(jnp.logical_and(has, has_l), pltpu.roll(halo(0)[1], 1, 0), 0.0)
                corner_r = jnp.where(jnp.logical_and(has, has_r), pltpu.roll(halo(2)[0], 7, 0), 0.0)
                v0, v1 = halo(1)
                store(jnp.where(has, v0, 0.0), jnp.where(has, v1, 0.0), corner_l, corner_r, tile, pair_at, half)

            def body(step, carry):
                r0 = step * ROW_BLOCK
                for at in range(ROW_BLOCK):
                    r = r0 + at
                    v0, v1 = row_source(s, r, tile)
                    v0, v1 = silu(v0, hs, ht), silu(v1, hs, ht)
                    from_left = jnp.broadcast_to(edge_l[pl.ds(r, 1), :], (8, LANES))
                    from_right = jnp.broadcast_to(edge_r[pl.ds(r, 1), :], (8, LANES))
                    store(v0, v1, from_left, from_right, tile, step * (ROW_BLOCK // 2) + (at + 1) // 2, (at + 1) % 2)
                return carry

            lax.fori_loop(0, rows // ROW_BLOCK, body, 0)

    def place_rest(pad, off, tile, pair_at, half, value):
        pad[off, pair_at, :, half * LANES:(half + 1) * LANES] = value

    def place_first(pad, off, tile, pair_at, half, value):
        pad[off, pair_at, half, :, tile * LANES:(tile + 1) * LANES] = value

    def act_rows(s, r, tile):
        row = act[s, r, :, tile * LANES:(tile + 1) * LANES].astype(jnp.float32)
        return row[0:8], row[8:16]

    def rows_of(ref):
        def source(s, r, tile):
            base = pl.multiple_of(r * cols, cols)
            return ref[s, pl.ds(base, 8), :], ref[s, pl.ds(base + 8, 8), :]
        return source

    zero = jnp.zeros((LANES, LANES), jnp.bfloat16)

    def square_of(a, b, c, d):
        return jnp.concatenate([jnp.concatenate([a, b], axis=1), jnp.concatenate([c, d], axis=1)], axis=0)

    def conv_rest(weight):
        total = None
        for off in range(3):
            w0, w1, w2 = (weight(row_off, off) for row_off in range(3))
            for shift, tap in ((0, square_of(w0, zero, w1, w0)), (1, square_of(w2, w1, zero, w2))):
                lhs = pad_rest[off, shift:shift + pairs].reshape(pairs * cols, 2 * LANES)
                part = jnp.dot(lhs, tap, preferred_element_type=jnp.float32)
                total = part if total is None else total + part
        return total

    def conv_first():
        wide = jnp.zeros((2 * LANES, LANES), jnp.bfloat16)
        total = None
        for off in range(3):
            w0, w1, w2 = (wf[row_off, off] for row_off in range(3))
            for at, (a, b) in enumerate(((w0, wide), (w1, w0), (w2, w1), (wide, w2))):
                lhs = pad_first[off, at // 2:at // 2 + pairs, at % 2].reshape(pairs * cols, 2 * LANES)
                part = jnp.dot(lhs, jnp.concatenate([a, b], axis=1), preferred_element_type=jnp.float32)
                total = part if total is None else total + part
        return total

    def finish(layer, s, total, bias, target, extra):
        next_layer = layer + 1
        acc = [[None, None], [None, None]]
        edges = {}
        for pair_at in range(pairs):
            for half in range(2):
                value = total[pair_at * cols:(pair_at + 1) * cols, half * LANES:(half + 1) * LANES] + bias
                base = (2 * pair_at + half) * cols
                if extra is not None:
                    value = value + extra[s, base:base + cols, :]
                packed = value.astype(jnp.bfloat16)
                value = packed.astype(jnp.float32)
                target[s, base:base + cols, :] = value
                if pair_at == 0 and half == 0:
                    rs_rest[layer, s, 0] = packed
                if pair_at == pairs - 1 and half == 1:
                    rs_rest[layer, s, 1] = packed
                one = value[0:8] + value[8:16]
                two = value[0:8] * value[0:8] + value[8:16] * value[8:16]
                for at, part in enumerate((one, two)):
                    acc[at][half] = part if acc[at][half] is None else acc[at][half] + part
        for side in range(2):
            column = target[s, pl.ds(side * (cols - 1), rows, stride=cols), :]
            cs_rest[layer, s, side] = column.astype(jnp.bfloat16)
        sums = [jnp.sum(acc[at][0] + acc[at][1], axis=0, keepdims=True) for at in range(2)]
        send_all(next_layer, s, [jnp.concatenate(sums, axis=0)])

    def first_sums(s, carry):
        wait_for(act.at[s], load_sem.at[s])

        def body(step, sums):
            sums = list(sums)
            for at in range(ROW_BLOCK):
                r = step * ROW_BLOCK + at
                for tile in range(2):
                    v0, v1 = act_rows(s, r, tile)
                    slab[0, tile, pl.ds(pl.multiple_of(r * 8, 8), 8), :] = v0
                    slab[1, tile, pl.ds(pl.multiple_of(r * 8, 8), 8), :] = v1
                    sums[2 * tile] = sums[2 * tile] + (v0 + v1)
                    sums[2 * tile + 1] = sums[2 * tile + 1] + (v0 * v0 + v1 * v1)
            return tuple(sums)

        sums = lax.fori_loop(0, rows // ROW_BLOCK, body, (jnp.zeros((8, LANES), jnp.float32),) * 4)
        for side in range(2):
            for tile in range(2):
                column = slab[side, tile, pl.ds(7 * side, rows, stride=8), :]
                cs_first[s, side, :, tile * LANES:(tile + 1) * LANES] = column.astype(jnp.bfloat16)
        sums = [jnp.sum(part, axis=0, keepdims=True) for part in sums]
        if carry == "first":
            pl.semaphore_wait(barrier, peers_n - 1)
        send_all(0, s, [jnp.concatenate(sums[0:2], axis=0), jnp.concatenate(sums[2:4], axis=0)])
        return carry

    first_sums(0, "first")
    lax.fori_loop(1, samples, first_sums, 0)

    bias = bias_rest[...].astype(jnp.float32)
    loads[samples].wait()

    def shortcut(s, carry):
        flat = act[s].reshape(rows * cols, 2 * LANES)
        skip[s] = jnp.dot(flat, ws[...], preferred_element_type=jnp.float32) + bias[6:7]
        return carry

    lax.fori_loop(0, samples, shortcut, 0)
    for tap in range(9):
        three = wo_ref[tap // 3, tap % 3].astype(jnp.float32)
        eight = jnp.concatenate([three, jnp.zeros((8 - three.shape[0], LANES), jnp.float32)], axis=0)
        wo[tap] = jnp.concatenate([eight] * 16, axis=0).T.astype(jnp.bfloat16)
    loads[samples + 1].wait()
    loads[samples + 2].wait()

    def layer_first(s, carry):
        activate(0, s, pad_first, act_rows, place_first)
        finish(0, s, conv_first(), bias[0:1], mid, None)
        return carry

    lax.fori_loop(0, samples, layer_first, 0)
    for layer in range(1, LAYERS - 1):
        source, target = (mid, hid) if layer % 2 else (hid, mid)
        extra = None if layer % 2 == 0 else (skip if layer == 1 else hid)

        def layer_rest(s, carry):
            activate(layer, s, pad_rest, rows_of(source), place_rest)
            total = conv_rest(lambda row_off, off: wr[layer - 1, row_off, off])
            finish(layer, s, total, bias[layer:layer + 1], target, extra)
            return carry

        lax.fori_loop(0, samples, layer_rest, 0)

    lane = lax.broadcasted_iota(jnp.int32, (rows, LANES), 1)
    out_bias = bias_out[...].astype(jnp.float32)

    def layer_last(s, carry):
        activate(LAYERS - 1, s, pad_rest, rows_of(hid), place_rest)
        total = conv_rest(lambda row_off, off: wo[3 * row_off + off])
        for pair_at in range(pairs):
            for half in range(2):
                base = (2 * pair_at + half) * cols
                mid[s, base:base + cols, :] = total[pair_at * cols:(pair_at + 1) * cols, half * LANES:(half + 1) * LANES]
        merged = mid[s, pl.ds(0, rows, stride=cols), :]
        for col in range(1, cols):
            merged = jnp.where(lane // 8 == col, mid[s, pl.ds(col, rows, stride=cols), :], merged)
        turn[...] = jnp.concatenate([merged] * (LANES // rows), axis=0).T
        for chan in range(y_ref.shape[1]):
            plane = turn[pl.ds(chan, cols, stride=8), :]
            y_ref[s, chan] = plane[:, 0:rows] + out_bias[0:1, chan:chan + 1]
        return carry

    lax.fori_loop(0, samples, layer_last, 0)

    for layer in range(LAYERS):
        wait_for(stat_ref(layer).at[:, pl.ds(1, peers_n - 1)], st_send.at[layer])
        wait_for(row_ref(layer), row_send.at[layer])
        wait_for(col_ref(layer), col_send.at[layer])


def solution(mesh):
    rows_n, cols_n = mesh.shape["sy"], mesh.shape["sx"]
    peers_n = rows_n * cols_n
    tile_spec = P("dp", "sy", "sx", None)
    replicated = P()

    def local_decode(act_in, norm_first, w_first, w_short, norm_rest, w_rest, bias_rest, w_out, bias_out):
        samples, rows, cols, wide = act_in.shape
        chans = w_short.shape[1]
        out_chans = w_out.shape[3]
        f32, bf16 = jnp.float32, jnp.bfloat16
        rest = LAYERS - 1
        whole = pl.BlockSpec(memory_space=pltpu.VMEM)
        there = pl.BlockSpec(memory_space=pl.ANY)
        image = pl.pallas_call(
            functools.partial(decode_kernel, rows_n, cols_n),
            name="decode",
            out_shape=jax.ShapeDtypeStruct((samples, out_chans, cols, rows), f32),
            in_specs=[there, whole, there, there, whole, there, whole, whole, whole],
            out_specs=whole,
            scratch_shapes=[
                pltpu.VMEM(act_in.shape, bf16),
                pltpu.VMEM(w_first.shape, bf16),
                pltpu.VMEM(w_short.shape, bf16),
                pltpu.VMEM(w_rest.shape, bf16),
                pltpu.VMEM((9, chans, LANES), bf16),
                pltpu.VMEM((samples, rows * cols, chans), f32),
                pltpu.VMEM((samples, rows * cols, chans), f32),
                pltpu.VMEM((samples, rows * cols, chans), f32),
                pltpu.VMEM((3, rows // 2 + 1, 2, cols, wide), bf16),
                pltpu.VMEM((3, rows // 2 + 1, cols, 2 * chans), bf16),
                pltpu.VMEM((2, 2, rows * 8, LANES), f32),
                pltpu.VMEM((rows, LANES), f32),
                pltpu.VMEM((rows, LANES), f32),
                pltpu.VMEM((LANES, LANES), f32),
                pltpu.VMEM((samples, peers_n, 2, wide), f32),
                pltpu.VMEM((rest, samples, peers_n, 2, chans), f32),
                pltpu.VMEM((samples, 6, cols, wide), bf16),
                pltpu.VMEM((rest, samples, 6, cols, chans), bf16),
                pltpu.VMEM((samples, 2, rows, wide), bf16),
                pltpu.VMEM((rest, samples, 2, rows, chans), bf16),
                pltpu.VMEM((samples, 2, rows, wide), bf16),
                pltpu.VMEM((rest, samples, 2, rows, chans), bf16),
                pltpu.VMEM((rest, samples, 2, cols, chans), bf16),
                pltpu.SemaphoreType.DMA((samples + 3,)),
                pltpu.SemaphoreType.DMA((LAYERS, samples)),
                pltpu.SemaphoreType.DMA((LAYERS, samples)),
                pltpu.SemaphoreType.DMA((LAYERS, samples)),
                pltpu.SemaphoreType.DMA((LAYERS,)),
                pltpu.SemaphoreType.DMA((LAYERS,)),
                pltpu.SemaphoreType.DMA((LAYERS,)),
            ],
            compiler_params=pltpu.CompilerParams(collective_id=0, has_side_effects=True, vmem_limit_bytes=60 * 1024 * 1024),
        )(act_in, norm_first, w_first, w_short, norm_rest, w_rest, bias_rest, jnp.transpose(w_out, (0, 1, 3, 2)), bias_out.reshape(1, out_chans))
        return jnp.transpose(image, (0, 3, 2, 1))

    return jax.shard_map(local_decode, mesh=mesh, in_specs=(tile_spec,) + (replicated,) * 8, out_specs=tile_spec, check_vma=False)
```

time: 584 us -> 70 us (0.12); the launches traced: 575 us -> 69.9 us
  blocking collectives: 321 us -> 0 us
  Pallas kernels: 0 us -> 68.3 us
  starting transfers between devices: 60 us -> 0 us
  matrix products: 50.1 us -> 0 us
  local copies, waits for them, and re-layouts: 50.7 us -> 1.54 us
  other arithmetic: 46.4 us -> 0 us
  waiting for transfers between devices: 44.5 us -> 0 us
    psum x7 -> x0, blocking collectives: 321 us -> none  [group_norm_act(): totals = lax.psum(jnp.stack([sum_one, sum_two], axis=-1), ('sy', 'sx'))]
    pallas_call x0 -> x1, Pallas kernels: none -> 68.3 us  [local_decode(): pl.pallas_call(functools.partial(decode_kernel, rows_n, cols_n), name='de...]
    ppermute x28 -> x0, starting transfers between devices: 60 us -> none  [the longest x7 18.5 us: add_border(): bottom_row = lax.ppermute(act_map[:, :1], 'sy', to_above)]
    conv_general_dilated x7 -> x0, matrix products: 47.4 us -> none  [conv_tile(): lax.conv_general_dilated(add_border(act_map), kernel, (1, 1), ((0, 0), (0...]
    ppermute x28 -> x0, waiting for transfers between devices: 44.5 us -> none  [the longest x7 27.9 us: add_border(): right_col = lax.ppermute(tall[:, :, :1], 'sx', to_left)]
    convert_element_type x10 -> x0, other arithmetic: 16.3 us -> none  [the longest x7 16.3 us: group_norm_act(): jax.nn.silu(act_map.astype(jnp.float32) * chan_scale[:, None, None, :] +...]
    conv_general_dilated x7 -> x0, other arithmetic: 14.2 us -> none  [conv_tile(): lax.conv_general_dilated(add_border(act_map), kernel, (1, 1), ((0, 0), (0...]
    square x3 -> x0, local copies, waits for them, and re-layouts: 11.2 us -> none  [group_norm_act(): jnp.square(act_map.astype(jnp.float32))]
  transfers between devices with their start and end apart: 28 -> 0, of which waited for: 20 -> 0; matrix products, arithmetic and copies ran while one was open for 0% -> 0% of each run, Pallas kernels for 0% -> 0%
where the time goes in v1:
time: 70 us; the launch traced here: 69.9 us
  Pallas kernels  68.3 us (98%)
  local copies, waits for them, and re-layouts  1.54 us (2%)
    pallas_call x1, Pallas kernels, local_decode(): pl.pallas_call(functools.partial(decode_kernel, rows_n, cols_n), name='de...  68.3 us
    unnamed x1, local copies, waits for them, and re-layouts  1.54 us

profile of v1, /device:TPU:97, one launch (start us, length us, event | category | flops | bytes accessed | tf_op | source)
XLA Modules:
  0.0 69.9 jit_solution(7052591239193401265)
XLA Ops:
  0.0 68.3 %decode.1 = f32[4,3,16,64]{3,2,1,0:T(8,128)} custom-call(bf16[4,64,16,256]{3,2,1,0:T(8,128)(2,1)} %act_hbm.1, bf16[2,256]{1,0:T(2,128)(2,1)} %norm_first.1, bf16[3,3,256,128]{3,2,1,0:T(8,128)(2,1)} %wf_hbm.1, bf16[256,128]{1,0:T(8,128)(2,1)} %ws_hbm.1, bf16[6,2,128]{2,1,0:T(2,128)(2,1)} %norm_rest.1, bf16[5,3,3,128,128]{4,3,2,1,0:T(8,128)(2,1)} %wr_hbm.1, ...), custom_call_target="tpu_custom_call" | custom-call | tf_op jit(solution)/shard_map/decode/pallas_call | solution.py:328
  68.4 1.5 %copy.11 = f32[4,64,16,3]{1,2,3,0:T(8,128)} copy(f32[4,64,16,3]{1,2,3,0:T(8,128)} %bitcast.3) | data formatting | bytes 98304

commit v2 on v0

v2 whole, which is shorter than its diff:
```python
import functools

import jax
import jax.numpy as jnp
from jax import lax
from jax.experimental import pallas as pl
from jax.experimental.pallas import tpu as pltpu
from jax.sharding import PartitionSpec as P

GROUPS = 32
GN_EPS = 1e-6
MESH = pl.DeviceIdType.MESH
LANES = 128
ROW_BLOCK = 8
LAYERS = 7
CHUNKS = 4


def group_total(vec, per_group):
    lane = lax.broadcasted_iota(jnp.int32, vec.shape, 1) & (per_group - 1)
    parts = [vec]
    for dist in range(1, per_group):
        parts.append(jnp.where(lane >= dist, pltpu.roll(vec, dist, 1), pltpu.roll(vec, LANES - per_group + dist, 1)))
    while len(parts) > 1:
        parts = [parts[at] + parts[at + 1] if at + 1 < len(parts) else parts[at] for at in range(0, len(parts), 2)]
    return parts[0]


def far_first(rows_n, cols_n):
    every = [(a, b) for a in range(cols_n) for b in range(rows_n) if a or b]
    return sorted(every, key=lambda off: -(min(off[0], cols_n - off[0]) + min(off[1], rows_n - off[1]) / 2))


def decode_kernel(rows_n, cols_n, act_hbm, norm_first, wf_hbm, ws_hbm, norm_rest, wr_hbm, bias_rest, wo_ref, bias_out, y_ref,
                  act, wf, ws, wr, wo, mid, hid, bias_rows, pad_first, pad_rest, slab, edge_l, edge_r, turn,
                  st_first, row_first, col_first, cs_first,
                  st_rest, corner_in, row_in, col_in, corner_out, row_out, col_out, whole_inbox,
                  load_sem, first_recv, col_recv, first_send, recv, send):
    samples, rows, cols, _ = act.shape
    pairs = rows // 2
    peers_n = rows_n * cols_n
    sx, sy = lax.axis_index("sx"), lax.axis_index("sy")
    at_x = [sx] + [lax.rem(sx + off, cols_n) for off in range(1, cols_n)]
    at_y = [sy] + [lax.rem(sy + off, rows_n) for off in range(1, rows_n)]
    order = far_first(rows_n, cols_n)
    has_l, has_r, has_t, has_b = sx > 0, sx < cols_n - 1, sy > 0, sy < rows_n - 1

    def device(off):
        return {"sx": at_x[off[0] % cols_n], "sy": at_y[off[1] % rows_n]}

    def wrap(off):
        return (off[0] % cols_n, off[1] % rows_n)

    corner_to = {wrap(off): at for at, off in enumerate(((-1, -1), (1, -1), (-1, 1), (1, 1)))}
    row_to = {wrap(off): at for at, off in enumerate(((0, -1), (0, 1)))}
    col_to = {wrap(off): at for at, off in enumerate(((-1, 0), (1, 0)))}
    plain = [off for off in order if off not in corner_to and off not in row_to and off not in col_to]

    loads = [pltpu.make_async_copy(act_hbm.at[s], act.at[s], load_sem.at[s]) for s in range(samples)]
    loads.append(pltpu.make_async_copy(ws_hbm, ws, load_sem.at[samples]))
    loads.append(pltpu.make_async_copy(wf_hbm, wf, load_sem.at[samples + 1]))
    loads.append(pltpu.make_async_copy(wr_hbm, wr, load_sem.at[samples + 2]))
    for load in loads:
        load.start()
    barrier = pltpu.get_barrier_semaphore()
    for off in order:
        pl.semaphore_signal(barrier, inc=1, device_id=device(off), device_id_type=MESH)

    def remote(src, dst, send_to, recv_at, off):
        pltpu.make_async_remote_copy(src_ref=src, dst_ref=dst, send_sem=send_to, recv_sem=recv_at, device_id=device(off), device_id_type=MESH).start()

    def wait_for(ref, sem):
        pltpu.make_async_copy(ref, ref, sem).wait()

    def send_rest(at, s):
        sem = recv.at[at, s]
        for off in order:
            if off in corner_to:
                box = corner_to[off]
                remote(corner_out.at[at, s, box], corner_in.at[at, s, 3 - box], send.at[1], sem, off)
            elif off in row_to:
                box = row_to[off]
                remote(row_out.at[at, s, box], row_in.at[at, s, 1 - box], send.at[2], sem, off)
            elif off in col_to:
                box = col_to[off]
                remote(col_out.at[at, s, box], col_in.at[at, s, 1 - box], send.at[3], sem, off)
            else:
                remote(st_rest.at[at, s, 0], st_rest.at[at, s, 1 + plain.index(off)], send.at[0], sem, off)

    sub = lax.broadcasted_iota(jnp.int32, (1, 8, LANES), 1)
    first_sub, last_sub = sub == 0, sub == 7

    def affine(total, norm, per_group):
        count = rows * rows_n * cols * cols_n * per_group
        mean = group_total(jnp.broadcast_to(total[0:1], (8, LANES)), per_group) / count
        square = group_total(jnp.broadcast_to(total[1:2], (8, LANES)), per_group) / count
        scale = lax.rsqrt(square - mean * mean + GN_EPS) * jnp.broadcast_to(norm[0:1], (8, LANES))
        shift = jnp.broadcast_to(norm[1:2], (8, LANES)) - mean * scale
        return 0.5 * scale, 0.5 * shift

    def silu(x, scales):
        u = x * scales[0] + scales[1]
        return u + u * jnp.tanh(u)

    def spread(rows_of_cols, from_left, from_right):
        v0, v1 = rows_of_cols[:, 0], rows_of_cols[:, 1]
        r0, r1 = pltpu.roll(v0, 1, 1), pltpu.roll(v1, 1, 1)
        q0, q1 = pltpu.roll(v0, 7, 1), pltpu.roll(v1, 7, 1)
        shifted = (
            (jnp.where(first_sub, from_left, r0), jnp.where(first_sub, r0, r1)),
            (v0, v1),
            (jnp.where(last_sub, q1, q0), jnp.where(last_sub, from_right, q1)),
        )
        return [jnp.concatenate(pair, axis=1).astype(jnp.bfloat16) for pair in shifted]

    def edges(tile, scales, halo_cols):
        one_row = (scales[0][0:1], scales[1][0:1])
        edge_l[tile] = jnp.where(has_l, silu(halo_cols[0], one_row), 0.0)
        edge_r[tile] = jnp.where(has_r, silu(halo_cols[1], one_row), 0.0)

    def activate(block, tile, scales, halo_rows, corners, row_source, place):
        begin, end = max(0, 8 * block + 1), min(rows, 8 * block + 9)
        value = row_source(begin, end)
        lefts = [jnp.broadcast_to(edge_l[tile, r:r + 1, :], (8, LANES)) for r in range(begin, end)]
        rights = [jnp.broadcast_to(edge_r[tile, r:r + 1, :], (8, LANES)) for r in range(begin, end)]
        value = silu(value, scales)
        for at, has in enumerate((has_t, has_b)):
            if block == (-1, rows // 8 - 1)[at]:
                halo = jnp.where(has, silu(halo_rows[at].reshape(1, 2, 8, LANES), scales), 0.0)
                corner_l = jnp.where(jnp.logical_and(has, has_l), silu(corners[2 * at], scales), 0.0)
                corner_r = jnp.where(jnp.logical_and(has, has_r), silu(corners[2 * at + 1], scales), 0.0)
                where_at = 0 if at == 0 else len(lefts)
                value = jnp.concatenate([halo, value] if at == 0 else [value, halo], axis=0)
                lefts.insert(where_at, corner_l)
                rights.insert(where_at, corner_r)
        for off, part in enumerate(spread(value, jnp.stack(lefts), jnp.stack(rights))):
            place(off, tile, 4 * block + 1 if block >= 0 else 0, part.reshape(part.shape[0] // 2, 2, cols, LANES))

    def prepare_rest(at, s, source):
        wait_for(whole_inbox, recv.at[at, s])
        total = jnp.sum(st_rest[at, s], axis=0)
        for box in range(4):
            total = total + corner_in[at, s, box, 0:2]
        for box in range(2):
            total = total + (row_in[at, s, box, 0:2] + col_in[at, s, box, 0:2])
        scales = affine(total, norm_rest[at].astype(jnp.float32), LANES // GROUPS)

        def row_source(begin, end):
            return source[s, begin * cols:end * cols, :].reshape(end - begin, 2, 8, LANES)

        def place(off, tile, pair_at, value):
            for half in range(2):
                pad_rest[off, pair_at:pair_at + value.shape[0], :, half * LANES:(half + 1) * LANES] = value[:, half]

        edges(0, scales, [col_in[at, s, box, 8:8 + rows, :] for box in range(2)])
        halo_rows = [row_in[at, s, box, 8:8 + cols, :] for box in range(2)]
        corners = [jnp.broadcast_to(corner_in[at, s, box, 2:3, :], (8, LANES)) for box in range(4)]
        return lambda block: activate(block, 0, scales, halo_rows, corners, row_source, place)

    def prepare_first(s):
        wait_for(col_first.at[s], col_recv.at[s])
        total = jnp.sum(st_first[:, s], axis=0)
        norm = norm_first[...].astype(jnp.float32)

        def one_tile(tile):
            lanes = slice(tile * LANES, (tile + 1) * LANES)
            scales = affine(total[:, lanes], norm[:, lanes], 2 * LANES // GROUPS)

            def row_source(begin, end):
                return act[s, begin:end, :, lanes].astype(jnp.float32).reshape(end - begin, 2, 8, LANES)

            def place(off, tile, pair_at, value):
                pad_first[off, pair_at:pair_at + value.shape[0], :, :, lanes] = value

            edges(tile, scales, [col_first[s, box, :, lanes].astype(jnp.float32) for box in range(2)])
            halo_rows = [row_first[box, s, :, lanes].astype(jnp.float32) for box in (1, 4)]
            corners = []
            for box in (0, 2, 3, 5):
                row = row_first[box, s, :, lanes].astype(jnp.float32)
                corners.append(pltpu.roll(row[8:16], 1, 0) if box % 3 == 0 else pltpu.roll(row[0:8], 7, 0))
            return lambda block: activate(block, tile, scales, halo_rows, corners, row_source, place)

        tiles = [one_tile(tile) for tile in range(2)]
        return lambda block: [tile(block) for tile in tiles]

    zero = jnp.zeros((LANES, LANES), jnp.bfloat16)
    wide_zero = jnp.zeros((2 * LANES, LANES), jnp.bfloat16)

    def square_of(a, b, c, d):
        return jnp.concatenate([jnp.concatenate([a, b], axis=1), jnp.concatenate([c, d], axis=1)], axis=0)

    def conv_rest(weight, pair_from, pair_n):
        total = None
        for off in range(3):
            w0, w1, w2 = (weight(row_off, off) for row_off in range(3))
            for shift, tap in ((0, square_of(w0, zero, w1, w0)), (1, square_of(w2, w1, zero, w2))):
                lhs = pad_rest[off, pair_from + shift:pair_from + shift + pair_n].reshape(pair_n * cols, 2 * LANES)
                part = jnp.dot(lhs, tap, preferred_element_type=jnp.float32)
                total = part if total is None else total + part
        return total

    def conv_first(pair_from, pair_n):
        total = None
        for off in range(3):
            w0, w1, w2 = (wf[row_off, off] for row_off in range(3))
            for at, (a, b) in enumerate(((w0, wide_zero), (w1, w0), (w2, w1), (wide_zero, w2))):
                begin = pair_from + at // 2
                lhs = pad_first[off, begin:begin + pair_n, at % 2].reshape(pair_n * cols, 2 * LANES)
                part = jnp.dot(lhs, jnp.concatenate([a, b], axis=1), preferred_element_type=jnp.float32)
                total = part if total is None else total + part
        return total

    def in_chunks(block, conv, use):
        block(-1)
        done, per_chunk = 0, pairs // CHUNKS
        for chunk in range(CHUNKS):
            while 4 * done < (chunk + 1) * per_chunk:
                block(done)
                done += 1
            total = conv(chunk * per_chunk, per_chunk)
            halves = [total[:, half * LANES:(half + 1) * LANES].reshape(per_chunk, 1, cols, LANES) for half in range(2)]
            use(2 * chunk * per_chunk, jnp.concatenate(halves, axis=1).reshape(2 * per_chunk * cols, LANES))

    def finish(at, s, block, conv, bias, target, residual):
        acc = []

        def use(row, value):
            rows_in = value.shape[0] // cols
            value = value + bias
            if residual is not None:
                value = value + residual[s, row * cols:row * cols + value.shape[0], :]
            value = value.astype(jnp.bfloat16).astype(jnp.float32)
            target[s, row * cols:row * cols + value.shape[0], :] = value
            for edge, edge_row in enumerate((0, rows - 1)):
                if row <= edge_row < row + rows_in:
                    line = value[(edge_row - row) * cols:(edge_row - row + 1) * cols]
                    row_out[at, s, edge, 8:8 + cols, :] = line
                    corner_out[at, s, 2 * edge, 2:3, :] = line[0:1]
                    corner_out[at, s, 2 * edge + 1, 2:3, :] = line[cols - 1:cols]
            split = value.reshape(value.shape[0] // 16, 2, 8, LANES)
            acc.append([jnp.sum(split, axis=0), jnp.sum(split * split, axis=0)])

        in_chunks(block, conv, use)
        sums = []
        for which in range(2):
            part = acc[0][which]
            for more in acc[1:]:
                part = part + more[which]
            sums.append(jnp.sum(part[0] + part[1], axis=0, keepdims=True))
        sums = jnp.concatenate(sums, axis=0)
        st_rest[at, s, 0] = sums
        for box in range(4):
            corner_out[at, s, box, 0:2, :] = sums
        for box in range(2):
            col_out[at, s, box, 8:8 + rows, :] = target[s, pl.ds(box * (cols - 1), rows, stride=cols), :]
            row_out[at, s, box, 0:2, :] = sums
            col_out[at, s, box, 0:2, :] = sums
        send_rest(at, s)

    def first_sums(s, carry):
        wait_for(act.at[s], load_sem.at[s])

        def body(step, sums):
            sums = list(sums)
            for at in range(ROW_BLOCK):
                r = step * ROW_BLOCK + at
                for tile in range(2):
                    row = act[s, r, :, tile * LANES:(tile + 1) * LANES].astype(jnp.float32)
                    v0, v1 = row[0:8], row[8:16]
                    slab[0, tile, pl.ds(pl.multiple_of(r * 8, 8), 8), :] = v0
                    slab[1, tile, pl.ds(pl.multiple_of(r * 8, 8), 8), :] = v1
                    sums[2 * tile] = sums[2 * tile] + (v0 + v1)
                    sums[2 * tile + 1] = sums[2 * tile + 1] + (v0 * v0 + v1 * v1)
            return tuple(sums)

        sums = lax.fori_loop(0, rows // ROW_BLOCK, body, (jnp.zeros((8, LANES), jnp.float32),) * 4)
        for side in range(2):
            for tile in range(2):
                column = slab[side, tile, pl.ds(7 * side, rows, stride=8), :]
                cs_first[s, side, :, tile * LANES:(tile + 1) * LANES] = column.astype(jnp.bfloat16)
        for tile in range(2):
            two = [jnp.sum(part, axis=0, keepdims=True) for part in sums[2 * tile:2 * tile + 2]]
            st_first[0, s, :, tile * LANES:(tile + 1) * LANES] = jnp.concatenate(two, axis=0)
        return carry

    lax.fori_loop(0, samples, first_sums, 0)
    pl.semaphore_wait(barrier, peers_n - 1)

    def first_columns(s, carry):
        for off, box in col_to.items():
            remote(cs_first.at[s, box], col_first.at[s, 1 - box], first_send.at[2], col_recv.at[s], off)
        return carry

    lax.fori_loop(0, samples, first_columns, 0)
    for slot, off in enumerate(order):
        remote(st_first.at[0], st_first.at[slot + 1], first_send.at[0], first_recv.at[0], off)
    for row, y_off, base in ((0, -1, 3), (rows - 1, 1, 0)):
        for x_off, at in ((-1, 2), (0, 1), (1, 0)):
            remote(act.at[:, row], row_first.at[base + at], first_send.at[1], first_recv.at[1], (x_off, y_off))

    bias = bias_rest[...].astype(jnp.float32)
    loads[samples].wait()

    def shortcut(s, carry):
        flat = act[s].reshape(rows * cols, 2 * LANES)
        hid[s] = jnp.dot(flat, ws[...], preferred_element_type=jnp.float32) + bias[6:7]
        return carry

    lax.fori_loop(0, samples, shortcut, 0)
    for tap in range(9):
        three = wo_ref[tap // 3, tap % 3].astype(jnp.float32)
        eight = jnp.concatenate([three, jnp.zeros((8 - three.shape[0], LANES), jnp.float32)], axis=0)
        wo[tap] = jnp.concatenate([eight] * 16, axis=0).T.astype(jnp.bfloat16)
    loads[samples + 1].wait()
    loads[samples + 2].wait()
    wait_for(st_first.at[pl.ds(1, peers_n - 1)], first_recv.at[0])
    wait_for(row_first, first_recv.at[1])

    def layer_first(s, carry):
        finish(0, s, prepare_first(s), conv_first, bias[0:1], mid, None)
        return carry

    lax.fori_loop(0, samples, layer_first, 0)

    def layer_rest(layer, source, target, residual):
        def one_sample(s, carry):
            block = prepare_rest(layer - 1, s, source)
            conv = functools.partial(conv_rest, lambda row_off, off: wr[layer - 1, row_off, off])
            finish(layer, s, block, conv, bias_rows[pl.ds(layer, 1), :], target, residual)
            return carry

        lax.fori_loop(0, samples, one_sample, 0)

    def layer_pair(step, carry):
        layer_rest(2 * step + 1, mid, hid, hid)
        layer_rest(2 * step + 2, hid, mid, None)
        return carry

    bias_rows[0:bias.shape[0], :] = bias
    lax.fori_loop(0, (LAYERS - 2) // 2, layer_pair, 0)
    layer_rest(LAYERS - 2, mid, hid, hid)

    lane = lax.broadcasted_iota(jnp.int32, (rows, LANES), 1)
    out_bias = bias_out[...].astype(jnp.float32)

    def layer_last(s, carry):
        def use(row, value):
            mid[s, row * cols:row * cols + value.shape[0], :] = value

        in_chunks(prepare_rest(LAYERS - 2, s, hid), functools.partial(conv_rest, lambda row_off, off: wo[3 * row_off + off]), use)
        merged = mid[s, pl.ds(0, rows, stride=cols), :]
        for col in range(1, cols):
            merged = jnp.where(lane // 8 == col, mid[s, pl.ds(col, rows, stride=cols), :], merged)
        turn[...] = jnp.concatenate([merged] * (LANES // rows), axis=0).T
        for chan in range(y_ref.shape[1]):
            plane = turn[pl.ds(chan, cols, stride=8), :]
            y_ref[s, chan] = plane[:, 0:rows] + out_bias[0:1, chan:chan + 1]
        return carry

    lax.fori_loop(0, samples, layer_last, 0)

    wait_for(st_first.at[pl.ds(1, peers_n - 1)], first_send.at[0])
    wait_for(row_first, first_send.at[1])
    wait_for(cs_first, first_send.at[2])
    wait_for(st_rest.at[:, :, pl.ds(1, len(plain))], send.at[0])
    wait_for(corner_out, send.at[1])
    wait_for(row_out, send.at[2])
    wait_for(col_out, send.at[3])


def solution(mesh):
    rows_n, cols_n = mesh.shape["sy"], mesh.shape["sx"]
    peers_n = rows_n * cols_n
    tile_spec = P("dp", "sy", "sx", None)
    replicated = P()

    def local_decode(act_in, norm_first, w_first, w_short, norm_rest, w_rest, bias_rest, w_out, bias_out):
        samples, rows, cols, wide = act_in.shape
        chans = w_short.shape[1]
        out_chans = w_out.shape[3]
        f32, bf16 = jnp.float32, jnp.bfloat16
        rest, plain_n = LAYERS - 1, peers_n - 9
        whole = pl.BlockSpec(memory_space=pltpu.VMEM)
        there = pl.BlockSpec(memory_space=pl.ANY)
        image = pl.pallas_call(
            functools.partial(decode_kernel, rows_n, cols_n),
            name="decode",
            out_shape=jax.ShapeDtypeStruct((samples, out_chans, cols, rows), f32),
            in_specs=[there, whole, there, there, whole, there, whole, whole, whole],
            out_specs=whole,
            scratch_shapes=[
                pltpu.VMEM(act_in.shape, bf16),
                pltpu.VMEM(w_first.shape, bf16),
                pltpu.VMEM(w_short.shape, bf16),
                pltpu.VMEM(w_rest.shape, bf16),
                pltpu.VMEM((9, chans, LANES), bf16),
                pltpu.VMEM((samples, rows * cols, chans), f32),
                pltpu.VMEM((samples, rows * cols, chans), f32),
                pltpu.VMEM((8, chans), f32),
                pltpu.VMEM((3, rows // 2 + 1, 2, cols, wide), bf16),
                pltpu.VMEM((3, rows // 2 + 1, cols, 2 * chans), bf16),
                pltpu.VMEM((2, 2, rows * 8, LANES), f32),
                pltpu.VMEM((2, rows, LANES), f32),
                pltpu.VMEM((2, rows, LANES), f32),
                pltpu.VMEM((LANES, LANES), f32),
                pltpu.VMEM((peers_n, samples, 2, wide), f32),
                pltpu.VMEM((6, samples, cols, wide), bf16),
                pltpu.VMEM((samples, 2, rows, wide), bf16),
                pltpu.VMEM((samples, 2, rows, wide), bf16),
                pltpu.VMEM((rest, samples, plain_n + 1, 2, chans), f32),
                pltpu.VMEM((rest, samples, 4, 4, chans), f32),
                pltpu.VMEM((rest, samples, 2, 8 + cols, chans), f32),
                pltpu.VMEM((rest, samples, 2, 8 + rows, chans), f32),
                pltpu.VMEM((rest, samples, 4, 4, chans), f32),
                pltpu.VMEM((rest, samples, 2, 8 + cols, chans), f32),
                pltpu.VMEM((rest, samples, 2, 8 + rows, chans), f32),
                pltpu.VMEM((plain_n + 8 + 16 + cols + rows, 2, chans), f32),
                pltpu.SemaphoreType.DMA((samples + 3,)),
                pltpu.SemaphoreType.DMA((2,)),
                pltpu.SemaphoreType.DMA((samples,)),
                pltpu.SemaphoreType.DMA((3,)),
                pltpu.SemaphoreType.DMA((rest, samples)),
                pltpu.SemaphoreType.DMA((4,)),
            ],
            compiler_params=pltpu.CompilerParams(collective_id=0, has_side_effects=True, vmem_limit_bytes=60 * 1024 * 1024),
        )(act_in, norm_first, w_first, w_short, norm_rest, w_rest, bias_rest, jnp.transpose(w_out, (0, 1, 3, 2)), bias_out.reshape(1, out_chans))
        return jnp.transpose(image, (0, 3, 2, 1))

    return jax.shard_map(local_decode, mesh=mesh, in_specs=(tile_spec,) + (replicated,) * 8, out_specs=tile_spec, check_vma=False)
```

time: 584 us -> 60.9 us (0.10); the launches traced: 575 us -> 60.8 us
  blocking collectives: 321 us -> 0 us
  starting transfers between devices: 60 us -> 0 us
  Pallas kernels: 0 us -> 59.2 us
  matrix products: 50.1 us -> 0 us
  local copies, waits for them, and re-layouts: 50.7 us -> 1.54 us
  other arithmetic: 46.4 us -> 0 us
  waiting for transfers between devices: 44.5 us -> 0 us
    psum x7 -> x0, blocking collectives: 321 us -> none  [group_norm_act(): totals = lax.psum(jnp.stack([sum_one, sum_two], axis=-1), ('sy', 'sx'))]
    ppermute x28 -> x0, starting transfers between devices: 60 us -> none  [the longest x7 18.5 us: add_border(): bottom_row = lax.ppermute(act_map[:, :1], 'sy', to_above)]
    pallas_call x0 -> x1, Pallas kernels: none -> 59.2 us  [local_decode(): pl.pallas_call(functools.partial(decode_kernel, rows_n, cols_n), name='de...]
    conv_general_dilated x7 -> x0, matrix products: 47.4 us -> none  [conv_tile(): lax.conv_general_dilated(add_border(act_map), kernel, (1, 1), ((0, 0), (0...]
    ppermute x28 -> x0, waiting for transfers between devices: 44.5 us -> none  [the longest x7 27.9 us: add_border(): right_col = lax.ppermute(tall[:, :, :1], 'sx', to_left)]
    convert_element_type x10 -> x0, other arithmetic: 16.3 us -> none  [the longest x7 16.3 us: group_norm_act(): jax.nn.silu(act_map.astype(jnp.float32) * chan_scale[:, None, None, :] +...]
    conv_general_dilated x7 -> x0, other arithmetic: 14.2 us -> none  [conv_tile(): lax.conv_general_dilated(add_border(act_map), kernel, (1, 1), ((0, 0), (0...]
    square x3 -> x0, local copies, waits for them, and re-layouts: 11.2 us -> none  [group_norm_act(): jnp.square(act_map.astype(jnp.float32))]
  transfers between devices with their start and end apart: 28 -> 0, of which waited for: 20 -> 0; matrix products, arithmetic and copies ran while one was open for 0% -> 0% of each run, Pallas kernels for 0% -> 0%
where the time goes in v2:
time: 60.9 us; the launch traced here: 60.8 us
  Pallas kernels  59.2 us (97%)
  local copies, waits for them, and re-layouts  1.54 us (3%)
    pallas_call x1, Pallas kernels, local_decode(): pl.pallas_call(functools.partial(decode_kernel, rows_n, cols_n), name='de...  59.2 us
    unnamed x1, local copies, waits for them, and re-layouts  1.54 us

profile of v2, /device:TPU:97, one launch (start us, length us, event | category | flops | bytes accessed | tf_op | source)
XLA Modules:
  0.0 60.8 jit_solution(4507477173701518211)
XLA Ops:
  0.0 59.2 %decode.1 = f32[4,3,16,64]{3,2,1,0:T(8,128)} custom-call(bf16[4,64,16,256]{3,2,1,0:T(8,128)(2,1)} %act_hbm.1, bf16[2,256]{1,0:T(2,128)(2,1)} %norm_first.1, bf16[3,3,256,128]{3,2,1,0:T(8,128)(2,1)} %wf_hbm.1, bf16[256,128]{1,0:T(8,128)(2,1)} %ws_hbm.1, bf16[6,2,128]{2,1,0:T(2,128)(2,1)} %norm_rest.1, bf16[5,3,3,128,128]{4,3,2,1,0:T(8,128)(2,1)} %wr_hbm.1, ...), custom_call_target="tpu_custom_call" | custom-call | tf_op jit(solution)/shard_map/decode/pallas_call | solution.py:385
  59.3 1.5 %copy.11 = f32[4,64,16,3]{1,2,3,0:T(8,128)} copy(f32[4,64,16,3]{1,2,3,0:T(8,128)} %bitcast.3) | data formatting | bytes 98304

commit v3 on v2

--- a/solution.py
+++ b/solution.py
@@ -31,8 +31,8 @@
     return sorted(every, key=lambda off: -(min(off[0], cols_n - off[0]) + min(off[1], rows_n - off[1]) / 2))
 
 
-def decode_kernel(rows_n, cols_n, act_hbm, norm_first, wf_hbm, ws_hbm, norm_rest, wr_hbm, bias_rest, wo_ref, bias_out, y_ref,
-                  act, wf, ws, wr, wo, mid, hid, bias_rows, pad_first, pad_rest, slab, edge_l, edge_r, turn,
+def decode_kernel(rows_n, cols_n, act_hbm, nf_hbm, wf_hbm, ws_hbm, nr_hbm, wr_hbm, br_hbm, wo_hbm, bo_hbm, y_ref,
+                  act, norm_first, wf, ws, norm_rest, wr, bias_rest, wo_ref, bias_out, sums_first, total_first, wo, mid, hid, bias_rows, pad_first, pad_rest, slab, edge_l, edge_r, turn,
                   st_first, row_first, col_first, cs_first,
                   st_rest, corner_in, row_in, col_in, corner_out, row_out, col_out, whole_inbox,
                   load_sem, first_recv, col_recv, first_send, recv, send):
@@ -57,9 +57,9 @@
     plain = [off for off in order if off not in corner_to and off not in row_to and off not in col_to]
 
     loads = [pltpu.make_async_copy(act_hbm.at[s], act.at[s], load_sem.at[s]) for s in range(samples)]
-    loads.append(pltpu.make_async_copy(ws_hbm, ws, load_sem.at[samples]))
-    loads.append(pltpu.make_async_copy(wf_hbm, wf, load_sem.at[samples + 1]))
-    loads.append(pltpu.make_async_copy(wr_hbm, wr, load_sem.at[samples + 2]))
+    others = ((ws_hbm, ws), (br_hbm, bias_rest), (wo_hbm, wo_ref), (nf_hbm, norm_first), (wf_hbm, wf), (wr_hbm, wr), (nr_hbm, norm_rest), (bo_hbm, bias_out))
+    for at, (src, dst) in enumerate(others):
+        loads.append(pltpu.make_async_copy(src, dst, load_sem.at[samples + at]))
     for load in loads:
         load.start()
     barrier = pltpu.get_barrier_semaphore()
@@ -90,13 +90,16 @@
     sub = lax.broadcasted_iota(jnp.int32, (1, 8, LANES), 1)
     first_sub, last_sub = sub == 0, sub == 7
 
-    def affine(total, norm, per_group):
+    def affine(one, two, norm, per_group):
         count = rows * rows_n * cols * cols_n * per_group
-        mean = group_total(jnp.broadcast_to(total[0:1], (8, LANES)), per_group) / count
-        square = group_total(jnp.broadcast_to(total[1:2], (8, LANES)), per_group) / count
+        mean = group_total(one, per_group) / count
+        square = group_total(two, per_group) / count
         scale = lax.rsqrt(square - mean * mean + GN_EPS) * jnp.broadcast_to(norm[0:1], (8, LANES))
         shift = jnp.broadcast_to(norm[1:2], (8, LANES)) - mean * scale
         return 0.5 * scale, 0.5 * shift
+
+    first_group = 2 * LANES // GROUPS
+    lane_in_group = lax.broadcasted_iota(jnp.int32, (8, LANES), 1) & (first_group - 1)
 
     def silu(x, scales):
         u = x * scales[0] + scales[1]
@@ -143,7 +146,8 @@
             total = total + corner_in[at, s, box, 0:2]
         for box in range(2):
             total = total + (row_in[at, s, box, 0:2] + col_in[at, s, box, 0:2])
-        scales = affine(total, norm_rest[at].astype(jnp.float32), LANES // GROUPS)
+        one, two = (jnp.broadcast_to(total[which:which + 1], (8, LANES)) for which in range(2))
+        scales = affine(one, two, norm_rest[at].astype(jnp.float32), LANES // GROUPS)
 
         def row_source(begin, end):
             return source[s, begin * cols:end * cols, :].reshape(end - begin, 2, 8, LANES)
@@ -159,12 +163,13 @@
 
     def prepare_first(s):
         wait_for(col_first.at[s], col_recv.at[s])
-        total = jnp.sum(st_first[:, s], axis=0)
         norm = norm_first[...].astype(jnp.float32)
 
         def one_tile(tile):
             lanes = slice(tile * LANES, (tile + 1) * LANES)
-            scales = affine(total[:, lanes], norm[:, lanes], 2 * LANES // GROUPS)
+            packed = jnp.broadcast_to(total_first[tile:tile + 1], (8, LANES))
+            one, two = (jnp.where(lane_in_group == which * samples + s, packed, 0.0) for which in range(2))
+            scales = affine(one, two, norm[:, lanes], first_group)
 
             def row_source(begin, end):
                 return act[s, begin:end, :, lanes].astype(jnp.float32).reshape(end - begin, 2, 8, LANES)
@@ -279,27 +284,32 @@
                 column = slab[side, tile, pl.ds(7 * side, rows, stride=8), :]
                 cs_first[s, side, :, tile * LANES:(tile + 1) * LANES] = column.astype(jnp.bfloat16)
         for tile in range(2):
-            two = [jnp.sum(part, axis=0, keepdims=True) for part in sums[2 * tile:2 * tile + 2]]
-            st_first[0, s, :, tile * LANES:(tile + 1) * LANES] = jnp.concatenate(two, axis=0)
+            for which in range(2):
+                sums_first[tile, pl.ds(which * samples + s, 1), :] = jnp.sum(sums[2 * tile + which], axis=0, keepdims=True)
         return carry
 
     lax.fori_loop(0, samples, first_sums, 0)
+    row_at = lax.broadcasted_iota(jnp.int32, (8, LANES), 0)
+    for tile in range(2):
+        grouped = jnp.where(row_at == lane_in_group, group_total(sums_first[tile], first_group), 0.0)
+        st_first[0, tile:tile + 1, :] = jnp.sum(grouped, axis=0, keepdims=True)
     pl.semaphore_wait(barrier, peers_n - 1)
-
-    def first_columns(s, carry):
-        for off, box in col_to.items():
-            remote(cs_first.at[s, box], col_first.at[s, 1 - box], first_send.at[2], col_recv.at[s], off)
-        return carry
-
-    lax.fori_loop(0, samples, first_columns, 0)
     for slot, off in enumerate(order):
         remote(st_first.at[0], st_first.at[slot + 1], first_send.at[0], first_recv.at[0], off)
     for row, y_off, base in ((0, -1, 3), (rows - 1, 1, 0)):
         for x_off, at in ((-1, 2), (0, 1), (1, 0)):
             remote(act.at[:, row], row_first.at[base + at], first_send.at[1], first_recv.at[1], (x_off, y_off))
 
+    def first_columns(s, carry):
+        for off, box in col_to.items():
+            remote(cs_first.at[s, box], col_first.at[s, 1 - box], first_send.at[2], col_recv.at[s], off)
+        return carry
+
+    lax.fori_loop(0, samples, first_columns, 0)
+
+    for load in loads[samples:samples + 3]:
+        load.wait()
     bias = bias_rest[...].astype(jnp.float32)
-    loads[samples].wait()
 
     def shortcut(s, carry):
         flat = act[s].reshape(rows * cols, 2 * LANES)
@@ -311,9 +321,10 @@
         three = wo_ref[tap // 3, tap % 3].astype(jnp.float32)
         eight = jnp.concatenate([three, jnp.zeros((8 - three.shape[0], LANES), jnp.float32)], axis=0)
         wo[tap] = jnp.concatenate([eight] * 16, axis=0).T.astype(jnp.bfloat16)
-    loads[samples + 1].wait()
-    loads[samples + 2].wait()
+    for load in loads[samples + 3:]:
+        load.wait()
     wait_for(st_first.at[pl.ds(1, peers_n - 1)], first_recv.at[0])
+    total_first[0:2, :] = jnp.sum(st_first[...], axis=0)
     wait_for(row_first, first_recv.at[1])
 
     def layer_first(s, carry):
@@ -381,18 +392,25 @@
         f32, bf16 = jnp.float32, jnp.bfloat16
         rest, plain_n = LAYERS - 1, peers_n - 9
         whole = pl.BlockSpec(memory_space=pltpu.VMEM)
-        there = pl.BlockSpec(memory_space=pl.ANY)
+        there = pl.BlockSpec(memory_space=pltpu.HBM)
         image = pl.pallas_call(
             functools.partial(decode_kernel, rows_n, cols_n),
             name="decode",
             out_shape=jax.ShapeDtypeStruct((samples, out_chans, cols, rows), f32),
-            in_specs=[there, whole, there, there, whole, there, whole, whole, whole],
+            in_specs=[there] * 9,
             out_specs=whole,
             scratch_shapes=[
                 pltpu.VMEM(act_in.shape, bf16),
+                pltpu.VMEM(norm_first.shape, bf16),
                 pltpu.VMEM(w_first.shape, bf16),
                 pltpu.VMEM(w_short.shape, bf16),
+                pltpu.VMEM(norm_rest.shape, bf16),
                 pltpu.VMEM(w_rest.shape, bf16),
+                pltpu.VMEM(bias_rest.shape, bf16),
+                pltpu.VMEM((3, 3, out_chans, chans), bf16),
+                pltpu.VMEM((1, out_chans), bf16),
+                pltpu.VMEM((2, 8, LANES), f32),
+                pltpu.VMEM((8, LANES), f32),
                 pltpu.VMEM((9, chans, LANES), bf16),
                 pltpu.VMEM((samples, rows * cols, chans), f32),
                 pltpu.VMEM((samples, rows * cols, chans), f32),
@@ -403,7 +421,7 @@
                 pltpu.VMEM((2, rows, LANES), f32),
                 pltpu.VMEM((2, rows, LANES), f32),
                 pltpu.VMEM((LANES, LANES), f32),
-                pltpu.VMEM((peers_n, samples, 2, wide), f32),
+                pltpu.VMEM((peers_n, 2, LANES), f32),
                 pltpu.VMEM((6, samples, cols, wide), bf16),
                 pltpu.VMEM((samples, 2, rows, wide), bf16),
                 pltpu.VMEM((samples, 2, rows, wide), bf16),
@@ -415,7 +433,7 @@
                 pltpu.VMEM((rest, samples, 2, 8 + cols, chans), f32),
                 pltpu.VMEM((rest, samples, 2, 8 + rows, chans), f32),
                 pltpu.VMEM((plain_n + 8 + 16 + cols + rows, 2, chans), f32),
-                pltpu.SemaphoreType.DMA((samples + 3,)),
+                pltpu.SemaphoreType.DMA((samples + 8,)),
                 pltpu.SemaphoreType.DMA((2,)),
                 pltpu.SemaphoreType.DMA((samples,)),
                 pltpu.SemaphoreType.DMA((3,)),

time: 60.9 us -> 57.5 us (0.944)
  Pallas kernels: 59.2 us -> 55.8 us
    pallas_call x1, Pallas kernels: 59.2 us -> 55.8 us  [local_decode(): pl.pallas_call(functools.partial(decode_kernel, rows_n, cols_n), name='de...]
where the time goes in v3:
time: 57.5 us; the launch traced here: 57.4 us
  Pallas kernels  55.8 us (97%)
  local copies, waits for them, and re-layouts  1.54 us (3%)
    pallas_call x1, Pallas kernels, local_decode(): pl.pallas_call(functools.partial(decode_kernel, rows_n, cols_n), name='de...  55.8 us
    unnamed x1, local copies, waits for them, and re-layouts  1.54 us

profile of v3, /device:TPU:97, one launch (start us, length us, event | category | flops | bytes accessed | tf_op | source)
XLA Modules:
  0.0 57.4 jit_solution(10113434646604849025)
XLA Ops:
  0.0 55.8 %decode.1 = f32[4,3,16,64]{3,2,1,0:T(8,128)} custom-call(bf16[4,64,16,256]{3,2,1,0:T(8,128)(2,1)} %act_hbm.1, bf16[2,256]{1,0:T(2,128)(2,1)} %nf_hbm.1, bf16[3,3,256,128]{3,2,1,0:T(8,128)(2,1)} %wf_hbm.1, bf16[256,128]{1,0:T(8,128)(2,1)} %ws_hbm.1, bf16[6,2,128]{2,1,0:T(2,128)(2,1)} %nr_hbm.1, bf16[5,3,3,128,128]{4,3,2,1,0:T(8,128)(2,1)} %wr_hbm.1, ...), custom_call_target="tpu_custom_call" | custom-call | tf_op jit(solution)/shard_map/decode/pallas_call | solution.py:396
  55.9 1.5 %copy.11 = f32[4,64,16,3]{1,2,3,0:T(8,128)} copy(f32[4,64,16,3]{1,2,3,0:T(8,128)} %bitcast.3) | data formatting | bytes 98304

commit v4 on v3

--- a/solution.py
+++ b/solution.py
@@ -60,7 +60,7 @@
     others = ((ws_hbm, ws), (br_hbm, bias_rest), (wo_hbm, wo_ref), (nf_hbm, norm_first), (wf_hbm, wf), (wr_hbm, wr), (nr_hbm, norm_rest), (bo_hbm, bias_out))
     for at, (src, dst) in enumerate(others):
         loads.append(pltpu.make_async_copy(src, dst, load_sem.at[samples + at]))
-    for load in loads:
+    for load in loads[:samples]:
         load.start()
     barrier = pltpu.get_barrier_semaphore()
     for off in order:
@@ -89,6 +89,13 @@
 
     sub = lax.broadcasted_iota(jnp.int32, (1, 8, LANES), 1)
     first_sub, last_sub = sub == 0, sub == 7
+
+    def tree_sum(stack):
+        while stack.shape[0] > 1:
+            half = stack.shape[0] // 2
+            folded = stack[:half] + stack[half:2 * half]
+            stack = folded if stack.shape[0] == 2 * half else jnp.concatenate([folded[:1] + stack[2 * half:], folded[1:]], axis=0) if half > 1 else folded + stack[2 * half:]
+        return stack[0]
 
     def affine(one, two, norm, per_group):
         count = rows * rows_n * cols * cols_n * per_group
@@ -141,11 +148,8 @@
 
     def prepare_rest(at, s, source):
         wait_for(whole_inbox, recv.at[at, s])
-        total = jnp.sum(st_rest[at, s], axis=0)
-        for box in range(4):
-            total = total + corner_in[at, s, box, 0:2]
-        for box in range(2):
-            total = total + (row_in[at, s, box, 0:2] + col_in[at, s, box, 0:2])
+        slots = [st_rest[at, s], corner_in[at, s, :, 0:2], row_in[at, s, :, 0:2], col_in[at, s, :, 0:2]]
+        total = tree_sum(jnp.concatenate(slots, axis=0))
         one, two = (jnp.broadcast_to(total[which:which + 1], (8, LANES)) for which in range(2))
         scales = affine(one, two, norm_rest[at].astype(jnp.float32), LANES // GROUPS)
 
@@ -289,6 +293,8 @@
         return carry
 
     lax.fori_loop(0, samples, first_sums, 0)
+    for load in loads[samples:]:
+        load.start()
     row_at = lax.broadcasted_iota(jnp.int32, (8, LANES), 0)
     for tile in range(2):
         grouped = jnp.where(row_at == lane_in_group, group_total(sums_first[tile], first_group), 0.0)
@@ -440,8 +446,8 @@
                 pltpu.SemaphoreType.DMA((rest, samples)),
                 pltpu.SemaphoreType.DMA((4,)),
             ],
-            compiler_params=pltpu.CompilerParams(collective_id=0, has_side_effects=True, vmem_limit_bytes=60 * 1024 * 1024),
-        )(act_in, norm_first, w_first, w_short, norm_rest, w_rest, bias_rest, jnp.transpose(w_out, (0, 1, 3, 2)), bias_out.reshape(1, out_chans))
+            compiler_params=pltpu.CompilerParams(collective_id=0, has_side_effects=True, vmem_limit_bytes=48 * 1024 * 1024),
+        )(*[pltpu.with_memory_space_constraint(x, pltpu.HBM) for x in (act_in, norm_first, w_first, w_short, norm_rest, w_rest, bias_rest, jnp.transpose(w_out, (0, 1, 3, 2)), bias_out.reshape(1, out_chans))])
         return jnp.transpose(image, (0, 3, 2, 1))
 
     return jax.shard_map(local_decode, mesh=mesh, in_specs=(tile_spec,) + (replicated,) * 8, out_specs=tile_spec, check_vma=False)

time: 57.5 us -> 55.5 us (0.965)
  Pallas kernels: 55.8 us -> 54.7 us
  local copies, waits for them, and re-layouts: 1.54 us -> 0.64 us
    pallas_call x1, Pallas kernels: 55.8 us -> 54.7 us  [local_decode(): pl.pallas_call(functools.partial(decode_kernel, rows_n, cols_n), name='de...]
    unnamed x1, local copies, waits for them, and re-layouts: 1.54 us -> 0.64 us
where the time goes in v4:
time: 55.5 us; the launch traced here: 55.4 us
  Pallas kernels  54.7 us (99%)
  local copies, waits for them, and re-layouts  0.64 us (1%)
    pallas_call x1, Pallas kernels, local_decode(): pl.pallas_call(functools.partial(decode_kernel, rows_n, cols_n), name='de...  54.7 us

profile of v4, /device:TPU:97, one launch (start us, length us, event | category | flops | bytes accessed | tf_op | source)
XLA Modules:
  0.0 55.4 jit_solution(15676955205169327054)
XLA Ops:
  0.0 54.7 %decode.1 = f32[4,3,16,64]{3,2,1,0:T(8,128)S(1)} custom-call(bf16[4,64,16,256]{3,2,1,0:T(8,128)(2,1)} %act_hbm.1, bf16[2,256]{1,0:T(2,128)(2,1)} %nf_hbm.1, bf16[3,3,256,128]{3,2,1,0:T(8,128)(2,1)} %wf_hbm.1, bf16[256,128]{1,0:T(8,128)(2,1)} %ws_hbm.1, bf16[6,2,128]{2,1,0:T(2,128)(2,1)} %nr_hbm.1, bf16[5,3,3,128,128]{4,3,2,1,0:T(8,128)(2,1)} %wr_hbm.1, ...), custom_call_target="tpu_custom_call" | custom-call | tf_op jit(solution)/shard_map/decode/pallas_call | solution.py:402
  54.7 0.6 %copy.11 = f32[4,64,16,3]{1,2,3,0:T(8,128)} copy(f32[4,64,16,3]{1,2,3,0:T(8,128)S(1)} %bitcast.3) | data formatting | bytes 98304

commit v5 on v4

--- a/solution.py
+++ b/solution.py
@@ -11,9 +11,10 @@
 GN_EPS = 1e-6
 MESH = pl.DeviceIdType.MESH
 LANES = 128
-ROW_BLOCK = 8
+ROW_BLOCK = 2
 LAYERS = 7
 CHUNKS = 4
+BLOCK = 2
 
 
 def group_total(vec, per_group):
@@ -121,7 +122,7 @@
             (v0, v1),
             (jnp.where(last_sub, q1, q0), jnp.where(last_sub, from_right, q1)),
         )
-        return [jnp.concatenate(pair, axis=1).astype(jnp.bfloat16) for pair in shifted]
+        return [jnp.concatenate(pair, axis=1) for pair in shifted]
 
     def edges(tile, scales, halo_cols):
         one_row = (scales[0][0:1], scales[1][0:1])
@@ -129,13 +130,13 @@
         edge_r[tile] = jnp.where(has_r, silu(halo_cols[1], one_row), 0.0)
 
     def activate(block, tile, scales, halo_rows, corners, row_source, place):
-        begin, end = max(0, 8 * block + 1), min(rows, 8 * block + 9)
+        begin, end = max(0, BLOCK * block + 1), min(rows, BLOCK * (block + 1) + 1)
         value = row_source(begin, end)
         lefts = [jnp.broadcast_to(edge_l[tile, r:r + 1, :], (8, LANES)) for r in range(begin, end)]
         rights = [jnp.broadcast_to(edge_r[tile, r:r + 1, :], (8, LANES)) for r in range(begin, end)]
         value = silu(value, scales)
         for at, has in enumerate((has_t, has_b)):
-            if block == (-1, rows // 8 - 1)[at]:
+            if block == (-1, rows // BLOCK - 1)[at]:
                 halo = jnp.where(has, silu(halo_rows[at].reshape(1, 2, 8, LANES), scales), 0.0)
                 corner_l = jnp.where(jnp.logical_and(has, has_l), silu(corners[2 * at], scales), 0.0)
                 corner_r = jnp.where(jnp.logical_and(has, has_r), silu(corners[2 * at + 1], scales), 0.0)
@@ -144,7 +145,7 @@
                 lefts.insert(where_at, corner_l)
                 rights.insert(where_at, corner_r)
         for off, part in enumerate(spread(value, jnp.stack(lefts), jnp.stack(rights))):
-            place(off, tile, 4 * block + 1 if block >= 0 else 0, part.reshape(part.shape[0] // 2, 2, cols, LANES))
+            place(off, tile, BLOCK // 2 * block + 1 if block >= 0 else 0, part.reshape(part.shape[0] // 2, 2, cols, LANES))
 
     def prepare_rest(at, s, source):
         wait_for(whole_inbox, recv.at[at, s])
@@ -204,7 +205,7 @@
             w0, w1, w2 = (weight(row_off, off) for row_off in range(3))
             for shift, tap in ((0, square_of(w0, zero, w1, w0)), (1, square_of(w2, w1, zero, w2))):
                 lhs = pad_rest[off, pair_from + shift:pair_from + shift + pair_n].reshape(pair_n * cols, 2 * LANES)
-                part = jnp.dot(lhs, tap, preferred_element_type=jnp.float32)
+                part = jnp.dot(lhs, tap.astype(jnp.float32), preferred_element_type=jnp.float32)
                 total = part if total is None else total + part
         return total
 
@@ -215,7 +216,7 @@
             for at, (a, b) in enumerate(((w0, wide_zero), (w1, w0), (w2, w1), (wide_zero, w2))):
                 begin = pair_from + at // 2
                 lhs = pad_first[off, begin:begin + pair_n, at % 2].reshape(pair_n * cols, 2 * LANES)
-                part = jnp.dot(lhs, jnp.concatenate([a, b], axis=1), preferred_element_type=jnp.float32)
+                part = jnp.dot(lhs, jnp.concatenate([a, b], axis=1).astype(jnp.float32), preferred_element_type=jnp.float32)
                 total = part if total is None else total + part
         return total
 
@@ -223,7 +224,7 @@
         block(-1)
         done, per_chunk = 0, pairs // CHUNKS
         for chunk in range(CHUNKS):
-            while 4 * done < (chunk + 1) * per_chunk:
+            while BLOCK // 2 * done < (chunk + 1) * per_chunk:
                 block(done)
                 done += 1
             total = conv(chunk * per_chunk, per_chunk)
@@ -421,8 +422,8 @@
                 pltpu.VMEM((samples, rows * cols, chans), f32),
                 pltpu.VMEM((samples, rows * cols, chans), f32),
                 pltpu.VMEM((8, chans), f32),
-                pltpu.VMEM((3, rows // 2 + 1, 2, cols, wide), bf16),
-                pltpu.VMEM((3, rows // 2 + 1, cols, 2 * chans), bf16),
+                pltpu.VMEM((3, rows // 2 + 1, 2, cols, wide), f32),
+                pltpu.VMEM((3, rows // 2 + 1, cols, 2 * chans), f32),
                 pltpu.VMEM((2, 2, rows * 8, LANES), f32),
                 pltpu.VMEM((2, rows, LANES), f32),
                 pltpu.VMEM((2, rows, LANES), f32),

time: 55.5 us -> 54.8 us (0.987)
  Pallas kernels: 54.7 us -> 54.1 us
    pallas_call x1, Pallas kernels: 54.7 us -> 54.1 us  [local_decode(): pl.pallas_call(functools.partial(decode_kernel, rows_n, cols_n), name='de...]
where the time goes in v5:
time: 54.8 us; the launch traced here: 54.7 us
  Pallas kernels  54.1 us (99%)
  local copies, waits for them, and re-layouts  0.64 us (1%)
    pallas_call x1, Pallas kernels, local_decode(): pl.pallas_call(functools.partial(decode_kernel, rows_n, cols_n), name='de...  54.1 us

profile of v5, /device:TPU:97, one launch (start us, length us, event | category | flops | bytes accessed | tf_op | source)
XLA Modules:
  0.0 54.7 jit_solution(15403259459167416631)
XLA Ops:
  0.0 54.1 %decode.1 = f32[4,3,16,64]{3,2,1,0:T(8,128)S(1)} custom-call(bf16[4,64,16,256]{3,2,1,0:T(8,128)(2,1)} %act_hbm.1, bf16[2,256]{1,0:T(2,128)(2,1)} %nf_hbm.1, bf16[3,3,256,128]{3,2,1,0:T(8,128)(2,1)} %wf_hbm.1, bf16[256,128]{1,0:T(8,128)(2,1)} %ws_hbm.1, bf16[6,2,128]{2,1,0:T(2,128)(2,1)} %nr_hbm.1, bf16[5,3,3,128,128]{4,3,2,1,0:T(8,128)(2,1)} %wr_hbm.1, ...), custom_call_target="tpu_custom_call" | custom-call | tf_op jit(solution)/shard_map/decode/pallas_call | solution.py:403
  54.1 0.6 %copy.11 = f32[4,64,16,3]{1,2,3,0:T(8,128)} copy(f32[4,64,16,3]{1,2,3,0:T(8,128)S(1)} %bitcast.3) | data formatting | bytes 98304

commit v6 on v5

--- a/solution.py
+++ b/solution.py
@@ -57,11 +57,17 @@
     col_to = {wrap(off): at for at, off in enumerate(((-1, 0), (1, 0)))}
     plain = [off for off in order if off not in corner_to and off not in row_to and off not in col_to]
 
-    loads = [pltpu.make_async_copy(act_hbm.at[s], act.at[s], load_sem.at[s]) for s in range(samples)]
+    half_rows = rows // 2
+    loads = []
+    for s in range(samples):
+        for half in range(2):
+            part = pl.ds(half * half_rows, half_rows)
+            loads.append(pltpu.make_async_copy(act_hbm.at[s, part], act.at[s, part], load_sem.at[2 * s + half]))
+    act_loads = 2 * samples
     others = ((ws_hbm, ws), (br_hbm, bias_rest), (wo_hbm, wo_ref), (nf_hbm, norm_first), (wf_hbm, wf), (wr_hbm, wr), (nr_hbm, norm_rest), (bo_hbm, bias_out))
     for at, (src, dst) in enumerate(others):
-        loads.append(pltpu.make_async_copy(src, dst, load_sem.at[samples + at]))
-    for load in loads[:samples]:
+        loads.append(pltpu.make_async_copy(src, dst, load_sem.at[act_loads + at]))
+    for load in loads[:act_loads]:
         load.start()
     barrier = pltpu.get_barrier_semaphore()
     for off in order:
@@ -73,20 +79,17 @@
     def wait_for(ref, sem):
         pltpu.make_async_copy(ref, ref, sem).wait()
 
-    def send_rest(at, s):
-        sem = recv.at[at, s]
-        for off in order:
-            if off in corner_to:
-                box = corner_to[off]
-                remote(corner_out.at[at, s, box], corner_in.at[at, s, 3 - box], send.at[1], sem, off)
-            elif off in row_to:
-                box = row_to[off]
-                remote(row_out.at[at, s, box], row_in.at[at, s, 1 - box], send.at[2], sem, off)
-            elif off in col_to:
-                box = col_to[off]
-                remote(col_out.at[at, s, box], col_in.at[at, s, 1 - box], send.at[3], sem, off)
-            else:
-                remote(st_rest.at[at, s, 0], st_rest.at[at, s, 1 + plain.index(off)], send.at[0], sem, off)
+    def send_plain(at, s):
+        for slot, off in enumerate(plain):
+            remote(st_rest.at[at, s, 0], st_rest.at[at, s, 1 + slot], send.at[0], recv.at[at, s], off)
+
+    def send_edges(at, s):
+        for off, box in corner_to.items():
+            remote(corner_out.at[at, s, box], corner_in.at[at, s, 3 - box], send.at[1], recv.at[at, s], off)
+        for off, box in col_to.items():
+            remote(col_out.at[at, s, box], col_in.at[at, s, 1 - box], send.at[3], recv.at[at, s], off)
+        for off, box in row_to.items():
+            remote(row_out.at[at, s, box], row_in.at[at, s, 1 - box], send.at[2], recv.at[at, s], off)
 
     sub = lax.broadcasted_iota(jnp.int32, (1, 8, LANES), 1)
     first_sub, last_sub = sub == 0, sub == 7
@@ -247,6 +250,9 @@
                     row_out[at, s, edge, 8:8 + cols, :] = line
                     corner_out[at, s, 2 * edge, 2:3, :] = line[0:1]
                     corner_out[at, s, 2 * edge + 1, 2:3, :] = line[cols - 1:cols]
+            for box in range(2):
+                column = target[s, pl.ds(row * cols + box * (cols - 1), rows_in, stride=cols), :]
+                col_out[at, s, box, 8 + row:8 + row + rows_in, :] = column
             split = value.reshape(value.shape[0] // 16, 2, 8, LANES)
             acc.append([jnp.sum(split, axis=0), jnp.sum(split * split, axis=0)])
 
@@ -259,16 +265,15 @@
             sums.append(jnp.sum(part[0] + part[1], axis=0, keepdims=True))
         sums = jnp.concatenate(sums, axis=0)
         st_rest[at, s, 0] = sums
+        send_plain(at, s)
         for box in range(4):
             corner_out[at, s, box, 0:2, :] = sums
         for box in range(2):
-            col_out[at, s, box, 8:8 + rows, :] = target[s, pl.ds(box * (cols - 1), rows, stride=cols), :]
             row_out[at, s, box, 0:2, :] = sums
             col_out[at, s, box, 0:2, :] = sums
-        send_rest(at, s)
+        send_edges(at, s)
 
     def first_sums(s, carry):
-        wait_for(act.at[s], load_sem.at[s])
 
         def body(step, sums):
             sums = list(sums)
@@ -283,7 +288,10 @@
                     sums[2 * tile + 1] = sums[2 * tile + 1] + (v0 * v0 + v1 * v1)
             return tuple(sums)
 
-        sums = lax.fori_loop(0, rows // ROW_BLOCK, body, (jnp.zeros((8, LANES), jnp.float32),) * 4)
+        sums = (jnp.zeros((8, LANES), jnp.float32),) * 4
+        for half in range(2):
+            wait_for(act.at[s, pl.ds(half * half_rows, half_rows)], load_sem.at[2 * s + half])
+            sums = lax.fori_loop(half * half_rows // ROW_BLOCK, (half + 1) * half_rows // ROW_BLOCK, body, sums)
         for side in range(2):
             for tile in range(2):
                 column = slab[side, tile, pl.ds(7 * side, rows, stride=8), :]
@@ -294,7 +302,7 @@
         return carry
 
     lax.fori_loop(0, samples, first_sums, 0)
-    for load in loads[samples:]:
+    for load in loads[act_loads:]:
         load.start()
     row_at = lax.broadcasted_iota(jnp.int32, (8, LANES), 0)
     for tile in range(2):
@@ -314,7 +322,7 @@
 
     lax.fori_loop(0, samples, first_columns, 0)
 
-    for load in loads[samples:samples + 3]:
+    for load in loads[act_loads:act_loads + 3]:
         load.wait()
     bias = bias_rest[...].astype(jnp.float32)
 
@@ -328,7 +336,7 @@
         three = wo_ref[tap // 3, tap % 3].astype(jnp.float32)
         eight = jnp.concatenate([three, jnp.zeros((8 - three.shape[0], LANES), jnp.float32)], axis=0)
         wo[tap] = jnp.concatenate([eight] * 16, axis=0).T.astype(jnp.bfloat16)
-    for load in loads[samples + 3:]:
+    for load in loads[act_loads + 3:]:
         load.wait()
     wait_for(st_first.at[pl.ds(1, peers_n - 1)], first_recv.at[0])
     total_first[0:2, :] = jnp.sum(st_first[...], axis=0)
@@ -440,7 +448,7 @@
                 pltpu.VMEM((rest, samples, 2, 8 + cols, chans), f32),
                 pltpu.VMEM((rest, samples, 2, 8 + rows, chans), f32),
                 pltpu.VMEM((plain_n + 8 + 16 + cols + rows, 2, chans), f32),
-                pltpu.SemaphoreType.DMA((samples + 8,)),
+                pltpu.SemaphoreType.DMA((2 * samples + 8,)),
                 pltpu.SemaphoreType.DMA((2,)),
                 pltpu.SemaphoreType.DMA((samples,)),
                 pltpu.SemaphoreType.DMA((3,)),

time: 54.8 us -> 54.6 us (level)
  no operation moved by 1% of the time
where the time goes in v6:
time: 54.6 us; the launch traced here: 54.5 us
  Pallas kernels  53.9 us (99%)
  local copies, waits for them, and re-layouts  0.64 us (1%)
    pallas_call x1, Pallas kernels, local_decode(): pl.pallas_call(functools.partial(decode_kernel, rows_n, cols_n), name='de...  53.9 us

profile of v6, /device:TPU:97, one launch (start us, length us, event | category | flops | bytes accessed | tf_op | source)
XLA Modules:
  0.0 54.5 jit_solution(9096371776005113988)
XLA Ops:
  0.0 53.9 %decode.1 = f32[4,3,16,64]{3,2,1,0:T(8,128)S(1)} custom-call(bf16[4,64,16,256]{3,2,1,0:T(8,128)(2,1)} %act_hbm.1, bf16[2,256]{1,0:T(2,128)(2,1)} %nf_hbm.1, bf16[3,3,256,128]{3,2,1,0:T(8,128)(2,1)} %wf_hbm.1, bf16[256,128]{1,0:T(8,128)(2,1)} %ws_hbm.1, bf16[6,2,128]{2,1,0:T(2,128)(2,1)} %nr_hbm.1, bf16[5,3,3,128,128]{4,3,2,1,0:T(8,128)(2,1)} %wr_hbm.1, ...), custom_call_target="tpu_custom_call" | custom-call | tf_op jit(solution)/shard_map/decode/pallas_call | solution.py:411
  53.9 0.6 %copy.11 = f32[4,64,16,3]{1,2,3,0:T(8,128)} copy(f32[4,64,16,3]{1,2,3,0:T(8,128)S(1)} %bitcast.3) | data formatting | bytes 98304

commit v7 on v6

--- a/solution.py
+++ b/solution.py
@@ -55,7 +55,7 @@
     corner_to = {wrap(off): at for at, off in enumerate(((-1, -1), (1, -1), (-1, 1), (1, 1)))}
     row_to = {wrap(off): at for at, off in enumerate(((0, -1), (0, 1)))}
     col_to = {wrap(off): at for at, off in enumerate(((-1, 0), (1, 0)))}
-    plain = [off for off in order if off not in corner_to and off not in row_to and off not in col_to]
+    plain = [off for off in order if off not in corner_to and off not in row_to]
 
     half_rows = rows // 2
     loads = []
@@ -152,7 +152,7 @@
 
     def prepare_rest(at, s, source):
         wait_for(whole_inbox, recv.at[at, s])
-        slots = [st_rest[at, s], corner_in[at, s, :, 0:2], row_in[at, s, :, 0:2], col_in[at, s, :, 0:2]]
+        slots = [st_rest[at, s], corner_in[at, s, :, 0:2], row_in[at, s, :, 0:2]]
         total = tree_sum(jnp.concatenate(slots, axis=0))
         one, two = (jnp.broadcast_to(total[which:which + 1], (8, LANES)) for which in range(2))
         scales = affine(one, two, norm_rest[at].astype(jnp.float32), LANES // GROUPS)
@@ -164,7 +164,7 @@
             for half in range(2):
                 pad_rest[off, pair_at:pair_at + value.shape[0], :, half * LANES:(half + 1) * LANES] = value[:, half]
 
-        edges(0, scales, [col_in[at, s, box, 8:8 + rows, :] for box in range(2)])
+        edges(0, scales, [col_in[at, s, box].astype(jnp.float32) for box in range(2)])
         halo_rows = [row_in[at, s, box, 8:8 + cols, :] for box in range(2)]
         corners = [jnp.broadcast_to(corner_in[at, s, box, 2:3, :], (8, LANES)) for box in range(4)]
         return lambda block: activate(block, 0, scales, halo_rows, corners, row_source, place)
@@ -252,7 +252,7 @@
                     corner_out[at, s, 2 * edge + 1, 2:3, :] = line[cols - 1:cols]
             for box in range(2):
                 column = target[s, pl.ds(row * cols + box * (cols - 1), rows_in, stride=cols), :]
-                col_out[at, s, box, 8 + row:8 + row + rows_in, :] = column
+                col_out[at, s, box, row:row + rows_in, :] = column.astype(jnp.bfloat16)
             split = value.reshape(value.shape[0] // 16, 2, 8, LANES)
             acc.append([jnp.sum(split, axis=0), jnp.sum(split * split, axis=0)])
 
@@ -270,7 +270,6 @@
             corner_out[at, s, box, 0:2, :] = sums
         for box in range(2):
             row_out[at, s, box, 0:2, :] = sums
-            col_out[at, s, box, 0:2, :] = sums
         send_edges(at, s)
 
     def first_sums(s, carry):
@@ -405,7 +404,7 @@
         chans = w_short.shape[1]
         out_chans = w_out.shape[3]
         f32, bf16 = jnp.float32, jnp.bfloat16
-        rest, plain_n = LAYERS - 1, peers_n - 9
+        rest, plain_n = LAYERS - 1, peers_n - 7
         whole = pl.BlockSpec(memory_space=pltpu.VMEM)
         there = pl.BlockSpec(memory_space=pltpu.HBM)
         image = pl.pallas_call(
@@ -443,11 +442,11 @@
                 pltpu.VMEM((rest, samples, plain_n + 1, 2, chans), f32),
                 pltpu.VMEM((rest, samples, 4, 4, chans), f32),
                 pltpu.VMEM((rest, samples, 2, 8 + cols, chans), f32),
-                pltpu.VMEM((rest, samples, 2, 8 + rows, chans), f32),
+                pltpu.VMEM((rest, samples, 2, rows, chans), bf16),
                 pltpu.VMEM((rest, samples, 4, 4, chans), f32),
                 pltpu.VMEM((rest, samples, 2, 8 + cols, chans), f32),
-                pltpu.VMEM((rest, samples, 2, 8 + rows, chans), f32),
-                pltpu.VMEM((plain_n + 8 + 16 + cols + rows, 2, chans), f32),
+                pltpu.VMEM((rest, samples, 2, rows, chans), bf16),
+                pltpu.VMEM((plain_n + 8 + 8 + cols + rows // 2, 2, chans), f32),
                 pltpu.SemaphoreType.DMA((2 * samples + 8,)),
                 pltpu.SemaphoreType.DMA((2,)),
                 pltpu.SemaphoreType.DMA((samples,)),

time: 54.6 us -> 55.3 us (1.013)
  Pallas kernels: 53.9 us -> 54.5 us
    pallas_call x1, Pallas kernels: 53.9 us -> 54.5 us  [local_decode(): pl.pallas_call(functools.partial(decode_kernel, rows_n, cols_n), name='de...]
where the time goes in v7:
time: 55.3 us; the launch traced here: 55.2 us
  Pallas kernels  54.5 us (99%)
  local copies, waits for them, and re-layouts  0.64 us (1%)
    pallas_call x1, Pallas kernels, local_decode(): pl.pallas_call(functools.partial(decode_kernel, rows_n, cols_n), name='de...  54.5 us

profile of v7, /device:TPU:97, one launch (start us, length us, event | category | flops | bytes accessed | tf_op | source)
XLA Modules:
  0.0 55.2 jit_solution(2542614816871275818)
XLA Ops:
  0.0 54.5 %decode.1 = f32[4,3,16,64]{3,2,1,0:T(8,128)S(1)} custom-call(bf16[4,64,16,256]{3,2,1,0:T(8,128)(2,1)} %act_hbm.1, bf16[2,256]{1,0:T(2,128)(2,1)} %nf_hbm.1, bf16[3,3,256,128]{3,2,1,0:T(8,128)(2,1)} %wf_hbm.1, bf16[256,128]{1,0:T(8,128)(2,1)} %ws_hbm.1, bf16[6,2,128]{2,1,0:T(2,128)(2,1)} %nr_hbm.1, bf16[5,3,3,128,128]{4,3,2,1,0:T(8,128)(2,1)} %wr_hbm.1, ...), custom_call_target="tpu_custom_call" | custom-call | tf_op jit(solution)/shard_map/decode/pallas_call | solution.py:410
  54.5 0.6 %copy.11 = f32[4,64,16,3]{1,2,3,0:T(8,128)} copy(f32[4,64,16,3]{1,2,3,0:T(8,128)S(1)} %bitcast.3) | data formatting | bytes 98304

commit v8 on v7

--- a/solution.py
+++ b/solution.py
@@ -11,10 +11,10 @@
 GN_EPS = 1e-6
 MESH = pl.DeviceIdType.MESH
 LANES = 128
-ROW_BLOCK = 2
+ROW_BLOCK = 8
 LAYERS = 7
 CHUNKS = 4
-BLOCK = 2
+BLOCK = 8
 
 
 def group_total(vec, per_group):
@@ -32,11 +32,15 @@
     return sorted(every, key=lambda off: -(min(off[0], cols_n - off[0]) + min(off[1], rows_n - off[1]) / 2))
 
 
+def is_far(off, rows_n, cols_n):
+    return min(off[0], cols_n - off[0]) + (min(off[1], rows_n - off[1]) + 1) // 2 > 2
+
+
 def decode_kernel(rows_n, cols_n, act_hbm, nf_hbm, wf_hbm, ws_hbm, nr_hbm, wr_hbm, br_hbm, wo_hbm, bo_hbm, y_ref,
                   act, norm_first, wf, ws, norm_rest, wr, bias_rest, wo_ref, bias_out, sums_first, total_first, wo, mid, hid, bias_rows, pad_first, pad_rest, slab, edge_l, edge_r, turn,
                   st_first, row_first, col_first, cs_first,
-                  st_rest, corner_in, row_in, col_in, corner_out, row_out, col_out, whole_inbox,
-                  load_sem, first_recv, col_recv, first_send, recv, send):
+                  st_rest, corner_in, row_in, col_in, corner_out, row_out, col_out, near_inbox,
+                  load_sem, first_recv, col_recv, first_send, recv, near_recv, send):
     samples, rows, cols, _ = act.shape
     pairs = rows // 2
     peers_n = rows_n * cols_n
@@ -56,6 +60,8 @@
     row_to = {wrap(off): at for at, off in enumerate(((0, -1), (0, 1)))}
     col_to = {wrap(off): at for at, off in enumerate(((-1, 0), (1, 0)))}
     plain = [off for off in order if off not in corner_to and off not in row_to]
+    plain.sort(key=lambda off: not is_far(off, rows_n, cols_n))
+    far_n = sum(is_far(off, rows_n, cols_n) for off in plain)
 
     half_rows = rows // 2
     loads = []
@@ -79,17 +85,21 @@
     def wait_for(ref, sem):
         pltpu.make_async_copy(ref, ref, sem).wait()
 
-    def send_plain(at, s):
+    def send_far(at, s):
+        for slot, off in enumerate(plain[:far_n]):
+            remote(st_rest.at[at, 0, s], st_rest.at[at, 1 + slot, s], send.at[0], recv.at[at, s], off)
+
+    def send_near(at, s):
+        both, sem = pl.ds(s - 1, 2), near_recv.at[at, s // 2]
+        for off, box in col_to.items():
+            remote(col_out.at[at, box, both], col_in.at[at, 1 - box, both], send.at[3], sem, off)
         for slot, off in enumerate(plain):
-            remote(st_rest.at[at, s, 0], st_rest.at[at, s, 1 + slot], send.at[0], recv.at[at, s], off)
-
-    def send_edges(at, s):
+            if slot >= far_n:
+                remote(st_rest.at[at, 0, both], st_rest.at[at, 1 + slot, both], send.at[0], sem, off)
         for off, box in corner_to.items():
-            remote(corner_out.at[at, s, box], corner_in.at[at, s, 3 - box], send.at[1], recv.at[at, s], off)
-        for off, box in col_to.items():
-            remote(col_out.at[at, s, box], col_in.at[at, s, 1 - box], send.at[3], recv.at[at, s], off)
+            remote(corner_out.at[at, box, both], corner_in.at[at, 3 - box, both], send.at[1], sem, off)
         for off, box in row_to.items():
-            remote(row_out.at[at, s, box], row_in.at[at, s, 1 - box], send.at[2], recv.at[at, s], off)
+            remote(row_out.at[at, box, both], row_in.at[at, 1 - box, both], send.at[2], sem, off)
 
     sub = lax.broadcasted_iota(jnp.int32, (1, 8, LANES), 1)
     first_sub, last_sub = sub == 0, sub == 7
@@ -151,8 +161,13 @@
             place(off, tile, BLOCK // 2 * block + 1 if block >= 0 else 0, part.reshape(part.shape[0] // 2, 2, cols, LANES))
 
     def prepare_rest(at, s, source):
-        wait_for(whole_inbox, recv.at[at, s])
-        slots = [st_rest[at, s], corner_in[at, s, :, 0:2], row_in[at, s, :, 0:2]]
+        wait_for(st_rest.at[at, pl.ds(1, far_n), s], recv.at[at, s])
+
+        @pl.when(lax.rem(s, 2) == 0)
+        def _():
+            wait_for(near_inbox, near_recv.at[at, s // 2])
+
+        slots = [st_rest[at, :, s], corner_in[at, :, s, 0:2], row_in[at, :, s, 0:2]]
         total = tree_sum(jnp.concatenate(slots, axis=0))
         one, two = (jnp.broadcast_to(total[which:which + 1], (8, LANES)) for which in range(2))
         scales = affine(one, two, norm_rest[at].astype(jnp.float32), LANES // GROUPS)
@@ -164,9 +179,9 @@
             for half in range(2):
                 pad_rest[off, pair_at:pair_at + value.shape[0], :, half * LANES:(half + 1) * LANES] = value[:, half]
 
-        edges(0, scales, [col_in[at, s, box].astype(jnp.float32) for box in range(2)])
-        halo_rows = [row_in[at, s, box, 8:8 + cols, :] for box in range(2)]
-        corners = [jnp.broadcast_to(corner_in[at, s, box, 2:3, :], (8, LANES)) for box in range(4)]
+        edges(0, scales, [col_in[at, box, s].astype(jnp.float32) for box in range(2)])
+        halo_rows = [row_in[at, box, s, 8:8 + cols, :] for box in range(2)]
+        corners = [jnp.broadcast_to(corner_in[at, box, s, 2:3, :], (8, LANES)) for box in range(4)]
         return lambda block: activate(block, 0, scales, halo_rows, corners, row_source, place)
 
     def prepare_first(s):
@@ -247,12 +262,12 @@
             for edge, edge_row in enumerate((0, rows - 1)):
                 if row <= edge_row < row + rows_in:
                     line = value[(edge_row - row) * cols:(edge_row - row + 1) * cols]
-                    row_out[at, s, edge, 8:8 + cols, :] = line
-                    corner_out[at, s, 2 * edge, 2:3, :] = line[0:1]
-                    corner_out[at, s, 2 * edge + 1, 2:3, :] = line[cols - 1:cols]
+                    row_out[at, edge, s, 8:8 + cols, :] = line
+                    corner_out[at, 2 * edge, s, 2:3, :] = line[0:1]
+                    corner_out[at, 2 * edge + 1, s, 2:3, :] = line[cols - 1:cols]
             for box in range(2):
                 column = target[s, pl.ds(row * cols + box * (cols - 1), rows_in, stride=cols), :]
-                col_out[at, s, box, row:row + rows_in, :] = column.astype(jnp.bfloat16)
+                col_out[at, box, s, row:row + rows_in, :] = column.astype(jnp.bfloat16)
             split = value.reshape(value.shape[0] // 16, 2, 8, LANES)
             acc.append([jnp.sum(split, axis=0), jnp.sum(split * split, axis=0)])
 
@@ -264,13 +279,13 @@
                 part = part + more[which]
             sums.append(jnp.sum(part[0] + part[1], axis=0, keepdims=True))
         sums = jnp.concatenate(sums, axis=0)
-        st_rest[at, s, 0] = sums
-        send_plain(at, s)
+        st_rest[at, 0, s] = sums
+        send_far(at, s)
         for box in range(4):
-            corner_out[at, s, box, 0:2, :] = sums
+            corner_out[at, box, s, 0:2, :] = sums
         for box in range(2):
-            row_out[at, s, box, 0:2, :] = sums
-        send_edges(at, s)
+            row_out[at, box, s, 0:2, :] = sums
+        pl.when(lax.rem(s, 2) == 1)(lambda: send_near(at, s))
 
     def first_sums(s, carry):
 
@@ -387,7 +402,7 @@
     wait_for(st_first.at[pl.ds(1, peers_n - 1)], first_send.at[0])
     wait_for(row_first, first_send.at[1])
     wait_for(cs_first, first_send.at[2])
-    wait_for(st_rest.at[:, :, pl.ds(1, len(plain))], send.at[0])
+    wait_for(st_rest.at[:, pl.ds(1, len(plain))], send.at[0])
     wait_for(corner_out, send.at[1])
     wait_for(row_out, send.at[2])
     wait_for(col_out, send.at[3])
@@ -405,6 +420,7 @@
         out_chans = w_out.shape[3]
         f32, bf16 = jnp.float32, jnp.bfloat16
         rest, plain_n = LAYERS - 1, peers_n - 7
+        far_n = sum(is_far(off, rows_n, cols_n) for off in far_first(rows_n, cols_n))
         whole = pl.BlockSpec(memory_space=pltpu.VMEM)
         there = pl.BlockSpec(memory_space=pltpu.HBM)
         image = pl.pallas_call(
@@ -439,19 +455,20 @@
                 pltpu.VMEM((6, samples, cols, wide), bf16),
                 pltpu.VMEM((samples, 2, rows, wide), bf16),
                 pltpu.VMEM((samples, 2, rows, wide), bf16),
-                pltpu.VMEM((rest, samples, plain_n + 1, 2, chans), f32),
-                pltpu.VMEM((rest, samples, 4, 4, chans), f32),
-                pltpu.VMEM((rest, samples, 2, 8 + cols, chans), f32),
-                pltpu.VMEM((rest, samples, 2, rows, chans), bf16),
-                pltpu.VMEM((rest, samples, 4, 4, chans), f32),
-                pltpu.VMEM((rest, samples, 2, 8 + cols, chans), f32),
-                pltpu.VMEM((rest, samples, 2, rows, chans), bf16),
-                pltpu.VMEM((plain_n + 8 + 8 + cols + rows // 2, 2, chans), f32),
+                pltpu.VMEM((rest, plain_n + 1, samples, 2, chans), f32),
+                pltpu.VMEM((rest, 4, samples, 4, chans), f32),
+                pltpu.VMEM((rest, 2, samples, 8 + cols, chans), f32),
+                pltpu.VMEM((rest, 2, samples, rows, chans), bf16),
+                pltpu.VMEM((rest, 4, samples, 4, chans), f32),
+                pltpu.VMEM((rest, 2, samples, 8 + cols, chans), f32),
+                pltpu.VMEM((rest, 2, samples, rows, chans), bf16),
+                pltpu.VMEM((2, plain_n - far_n + 8 + 8 + cols + rows // 2, 2, chans), f32),
                 pltpu.SemaphoreType.DMA((2 * samples + 8,)),
                 pltpu.SemaphoreType.DMA((2,)),
                 pltpu.SemaphoreType.DMA((samples,)),
                 pltpu.SemaphoreType.DMA((3,)),
                 pltpu.SemaphoreType.DMA((rest, samples)),
+                pltpu.SemaphoreType.DMA((rest, samples // 2)),
                 pltpu.SemaphoreType.DMA((4,)),
             ],
             compiler_params=pltpu.CompilerParams(collective_id=0, has_side_effects=True, vmem_limit_bytes=48 * 1024 * 1024),

time: 55.3 us -> 59.1 us (1.069)
  Pallas kernels: 54.5 us -> 58.3 us
    pallas_call x1, Pallas kernels: 54.5 us -> 58.3 us  [local_decode(): pl.pallas_call(functools.partial(decode_kernel, rows_n, cols_n), name='de...]
where the time goes in v8:
time: 59.1 us; the launch traced here: 59 us
  Pallas kernels  58.3 us (99%)
  local copies, waits for them, and re-layouts  0.64 us (1%)
    pallas_call x1, Pallas kernels, local_decode(): pl.pallas_call(functools.partial(decode_kernel, rows_n, cols_n), name='de...  58.3 us

profile of v8, /device:TPU:97, one launch (start us, length us, event | category | flops | bytes accessed | tf_op | source)
XLA Modules:
  0.0 59.0 jit_solution(5965604444659283951)
XLA Ops:
  0.0 58.3 %decode.1 = f32[4,3,16,64]{3,2,1,0:T(8,128)S(1)} custom-call(bf16[4,64,16,256]{3,2,1,0:T(8,128)(2,1)} %act_hbm.1, bf16[2,256]{1,0:T(2,128)(2,1)} %nf_hbm.1, bf16[3,3,256,128]{3,2,1,0:T(8,128)(2,1)} %wf_hbm.1, bf16[256,128]{1,0:T(8,128)(2,1)} %ws_hbm.1, bf16[6,2,128]{2,1,0:T(2,128)(2,1)} %nr_hbm.1, bf16[5,3,3,128,128]{4,3,2,1,0:T(8,128)(2,1)} %wr_hbm.1, ...), custom_call_target="tpu_custom_call" | custom-call | tf_op jit(solution)/shard_map/decode/pallas_call | solution.py:426
  58.3 0.6 %copy.11 = f32[4,64,16,3]{1,2,3,0:T(8,128)} copy(f32[4,64,16,3]{1,2,3,0:T(8,128)S(1)} %bitcast.3) | data formatting | bytes 98304

commit v9 on v6

--- a/solution.py
+++ b/solution.py
@@ -13,7 +13,7 @@
 LANES = 128
 ROW_BLOCK = 2
 LAYERS = 7
-CHUNKS = 4
+CHUNKS = (10, 12, 10)
 BLOCK = 2
 
 
@@ -225,14 +225,16 @@
 
     def in_chunks(block, conv, use):
         block(-1)
-        done, per_chunk = 0, pairs // CHUNKS
-        for chunk in range(CHUNKS):
-            while BLOCK // 2 * done < (chunk + 1) * per_chunk:
+        done, begin = 0, 0
+        for chunk in CHUNKS:
+            per_chunk = chunk * pairs // sum(CHUNKS)
+            while BLOCK // 2 * done < begin + per_chunk:
                 block(done)
                 done += 1
-            total = conv(chunk * per_chunk, per_chunk)
+            total = conv(begin, per_chunk)
             halves = [total[:, half * LANES:(half + 1) * LANES].reshape(per_chunk, 1, cols, LANES) for half in range(2)]
-            use(2 * chunk * per_chunk, jnp.concatenate(halves, axis=1).reshape(2 * per_chunk * cols, LANES))
+            use(2 * begin, jnp.concatenate(halves, axis=1).reshape(2 * per_chunk * cols, LANES))
+            begin += per_chunk
 
     def finish(at, s, block, conv, bias, target, residual):
         acc = []

time: 54.6 us -> 54.3 us (level)
  no operation moved by 1% of the time
where the time goes in v9:
time: 54.3 us
  Pallas kernels  53.6 us (99%)
  local copies, waits for them, and re-layouts  0.64 us (1%)
    pallas_call x1, Pallas kernels, local_decode(): pl.pallas_call(functools.partial(decode_kernel, rows_n, cols_n), name='de...  53.6 us

profile of v9, /device:TPU:97, one launch (start us, length us, event | category | flops | bytes accessed | tf_op | source)
XLA Modules:
  0.0 54.3 jit_solution(5747713386124077794)
XLA Ops:
  0.0 53.6 %decode.1 = f32[4,3,16,64]{3,2,1,0:T(8,128)S(1)} custom-call(bf16[4,64,16,256]{3,2,1,0:T(8,128)(2,1)} %act_hbm.1, bf16[2,256]{1,0:T(2,128)(2,1)} %nf_hbm.1, bf16[3,3,256,128]{3,2,1,0:T(8,128)(2,1)} %wf_hbm.1, bf16[256,128]{1,0:T(8,128)(2,1)} %ws_hbm.1, bf16[6,2,128]{2,1,0:T(2,128)(2,1)} %nr_hbm.1, bf16[5,3,3,128,128]{4,3,2,1,0:T(8,128)(2,1)} %wr_hbm.1, ...), custom_call_target="tpu_custom_call" | custom-call | tf_op jit(solution)/shard_map/decode/pallas_call | solution.py:413
  53.6 0.6 %copy.11 = f32[4,64,16,3]{1,2,3,0:T(8,128)} copy(f32[4,64,16,3]{1,2,3,0:T(8,128)S(1)} %bitcast.3) | data formatting | bytes 98304

commit v10 on v9

--- a/solution.py
+++ b/solution.py
@@ -13,7 +13,7 @@
 LANES = 128
 ROW_BLOCK = 2
 LAYERS = 7
-CHUNKS = (10, 12, 10)
+CHUNKS = (11, 11, 10)
 BLOCK = 2
 
 

time: 54.3 us -> 54.2 us (level)
  no operation moved by 1% of the time
where the time goes in v10:
time: 54.2 us; the launch traced here: 54.1 us
  Pallas kernels  53.5 us (99%)
  local copies, waits for them, and re-layouts  0.64 us (1%)
    pallas_call x1, Pallas kernels, local_decode(): pl.pallas_call(functools.partial(decode_kernel, rows_n, cols_n), name='de...  53.5 us

profile of v10, /device:TPU:97, one launch (start us, length us, event | category | flops | bytes accessed | tf_op | source)
XLA Modules:
  0.0 54.1 jit_solution(6826496074282552872)
XLA Ops:
  0.0 53.5 %decode.1 = f32[4,3,16,64]{3,2,1,0:T(8,128)S(1)} custom-call(bf16[4,64,16,256]{3,2,1,0:T(8,128)(2,1)} %act_hbm.1, bf16[2,256]{1,0:T(2,128)(2,1)} %nf_hbm.1, bf16[3,3,256,128]{3,2,1,0:T(8,128)(2,1)} %wf_hbm.1, bf16[256,128]{1,0:T(8,128)(2,1)} %ws_hbm.1, bf16[6,2,128]{2,1,0:T(2,128)(2,1)} %nr_hbm.1, bf16[5,3,3,128,128]{4,3,2,1,0:T(8,128)(2,1)} %wr_hbm.1, ...), custom_call_target="tpu_custom_call" | custom-call | tf_op jit(solution)/shard_map/decode/pallas_call | solution.py:413
  53.5 0.6 %copy.11 = f32[4,64,16,3]{1,2,3,0:T(8,128)} copy(f32[4,64,16,3]{1,2,3,0:T(8,128)S(1)} %bitcast.3) | data formatting | bytes 98304
